TPU v7x, 32 devices: a whole 2x2x4 slice. The times are simulated.
32 devices in a mesh: parts: 2 (over x), frame: 2 (over core), tile: 8 (over z, y).
Axes of the slice: x: 2, y: 2, z: 4, core: 2. Of those that a mesh axis runs over, the one named last changes fastest.
Arguments:
- decoded_refs: bfloat16 [64, 96, 64, 256], P(('parts', 'frame'), None, 'tile'), parts along dimension 0, may hold values from -6 to 6
- current_frames: bfloat16 [16, 96, 64, 256], P(('parts', 'frame'), None, 'tile'), parts along dimension 0, may hold values from -6 to 6
- ref_pairs: int32 [16, 2], P('parts'), parts along dimension 0, may hold values from 0 to 31
- ref_slots: int32 [64], P('parts'), parts along dimension 0, may hold values from 0 to 31, each once
- frame_numbers: int32 [16], P('parts'), parts along dimension 0, may hold values from 0 to 31
- rate_weights: float32 [64], P('parts'), parts along dimension 0, may hold values from 0.5 to 4
- join_kernel: bfloat16 [3, 3, 96, 288], replicated, may hold values from -0.125 to 0.125
- out_kernel: bfloat16 [3, 3, 96, 96], replicated, may hold values from -0.21875 to 0.21875
Outputs:
- reconstruction: bfloat16 [16, 96, 64, 256], P(('parts', 'frame'), None, 'tile'), parts along dimension 0
- join_grad: float32 [6, 3, 96, 288], P('parts'), parts along dimension 0
- output_grad: float32 [6, 3, 96, 96], P('parts'), parts along dimension 0
There are 2 independent parts, one for each index of `parts`. A program takes and returns all parts, laid end to end along the dimension named above; an argument that names none is the same for every part. Nothing has to cross between parts.
Inputs may be any that keep to these rules, and one draw needn't show every extreme that they name: `ref_pairs`: each B-frame names two decoded frames, possibly the same one. `ref_slots`: each slot holds exactly one decoded frame.
All inputs are finite; a program needn't handle non-finite values.
Results may differ from a plain program's by a relative error of at most 0.005.
Values may be sent and summed in bfloat16 or wider, within the bound.
A program may use at most 128 MiB of HBM per device.

v0:
```python
import jax
import jax.numpy as jnp
from jax import lax
from jax.sharding import PartitionSpec as P


def partner(array, axis, stride):
    return lax.ppermute(array, axis, [(i, i ^ 1 << stride) for i in range(lax.axis_size(axis))])


def with_halo(cells, sides, width):
    for axis, dim in sides:
        count = lax.axis_size(axis)
        ends = count - 1
        head = lax.slice_in_dim(cells, 0, width, axis=dim)
        tail = lax.slice_in_dim(cells, cells.shape[dim] - width, cells.shape[dim], axis=dim)
        cells = jnp.concatenate(
            [
                lax.ppermute(tail, axis, [(i, (i + 1) % count) for i in range(ends)]),
                cells,
                lax.ppermute(head, axis, [((i + 1) % count, i) for i in range(ends)]),
            ],
            axis=dim,
        )
    return cells


def pad_cols(field):
    return jnp.pad(field, ((0, 0), (0, 0), (0, 0), (1, 1)))


def apply_taps(padded, kernel, row_count, col_count):
    running = None
    for row_tap in range(3):
        for col_tap in range(3):
            window = padded[:, :, row_tap : row_tap + row_count, col_tap : col_tap + col_count]
            partial_sum = jnp.einsum(
                "oi,bihw->bohw",
                kernel[row_tap, col_tap],
                window,
                preferred_element_type=jnp.float32,
            )
            running = partial_sum if running is None else running + partial_sum
    return running


def tap_grads(upstream, padded, row_count, col_count):
    pieces = []
    for row_tap in range(3):
        for col_tap in range(3):
            window = padded[:, :, row_tap : row_tap + row_count, col_tap : col_tap + col_count]
            pieces.append(
                jnp.einsum("bohw,bihw->oi", upstream, window, preferred_element_type=jnp.float32)
            )
    stacked = jnp.stack(pieces)
    return stacked.reshape((3, 3) + stacked.shape[1:])


def transpose_taps(padded, kernel, row_count, col_count):
    running = None
    for row_tap in range(3):
        for col_tap in range(3):
            window = padded[
                :, :, 2 - row_tap : 2 - row_tap + row_count, 2 - col_tap : 2 - col_tap + col_count
            ]
            partial_sum = jnp.einsum(
                "oi,bohw->bihw",
                kernel[row_tap, col_tap],
                window,
                preferred_element_type=jnp.float32,
            )
            running = partial_sum if running is None else running + partial_sum
    return running


def on_device(
    decoded_refs,
    current_frames,
    ref_pairs,
    ref_slots,
    frame_numbers,
    rate_weights,
    join_kernel,
    out_kernel,
):
    local_refs = decoded_refs.shape[0]
    local_frames, channels, tile_rows, col_count = current_frames.shape
    group = lax.axis_index("frame")
    frame_range = jnp.arange(ref_slots.shape[0], dtype=jnp.int32)

    def pair_slots(which):
        pairs = lax.dynamic_slice_in_dim(ref_pairs, which * local_frames, local_frames, 0)
        return jnp.sum(jnp.where(pairs[:, :, None] == frame_range, ref_slots, 0), axis=-1).reshape(
            -1
        )

    mine = pair_slots(group)
    other = pair_slots(1 - group) - group * local_refs
    other_held = (other >= 0) & (other < local_refs)
    outgoing = jnp.take(decoded_refs, jnp.clip(other, 0, local_refs - 1), axis=0)
    outgoing = jnp.where(other_held[:, None, None, None], outgoing, jnp.zeros((), jnp.bfloat16))
    incoming = partner(outgoing, "frame", 0)
    mine_local = mine - group * local_refs
    mine_held = (mine_local >= 0) & (mine_local < local_refs)
    own_tiles = jnp.take(decoded_refs, jnp.clip(mine_local, 0, local_refs - 1), axis=0)
    picked = jnp.where(mine_held[:, None, None, None], own_tiles, incoming)
    picked = picked.reshape(local_frames, 2 * channels, tile_rows, col_count)
    stacked = jnp.concatenate([picked, current_frames], axis=1)
    height = tile_rows * lax.axis_size("tile")
    stacked_pad = pad_cols(with_halo(stacked, (("tile", 2),), 1))
    preact = apply_taps(stacked_pad, join_kernel, tile_rows, col_count)
    hidden = jax.nn.silu(preact).astype(jnp.bfloat16)
    hidden_pad = pad_cols(with_halo(hidden, (("tile", 2),), 1))
    recon = apply_taps(hidden_pad, out_kernel, tile_rows, col_count)
    frames_here = lax.dynamic_slice_in_dim(frame_numbers, group * local_frames, local_frames, 0)
    gop_range = jnp.arange(rate_weights.shape[0], dtype=jnp.int32)
    weight_here = jnp.sum(jnp.where(frames_here[:, None] == gop_range, rate_weights, 0.0), axis=-1)
    residual = (
        2.0
        * weight_here[:, None, None, None]
        * (recon - current_frames.astype(jnp.float32))
        / (height * col_count)
    ).astype(jnp.bfloat16)
    output_part = tap_grads(residual, hidden_pad, tile_rows, col_count)
    residual_pad = pad_cols(with_halo(residual, (("tile", 2),), 1))
    hidden_grad = transpose_taps(residual_pad, out_kernel, tile_rows, col_count)
    sigma = jax.nn.sigmoid(preact)
    preact_grad = (hidden_grad * (sigma * (1.0 + preact * (1.0 - sigma)))).astype(jnp.bfloat16)
    join_part = tap_grads(preact_grad, stacked_pad, tile_rows, col_count)
    join_total, output_total = lax.psum((join_part, output_part), ("frame", "tile"))
    return (recon.astype(jnp.bfloat16), join_total, output_total)


def solution(mesh):
    placed = (
        P(("parts", "frame"), None, "tile", None),
        P(("parts", "frame"), None, "tile", None),
        P("parts", None),
        P("parts"),
        P("parts"),
        P("parts"),
        P(),
        P(),
    )
    return jax.shard_map(
        on_device,
        mesh=mesh,
        in_specs=placed,
        out_specs=(
            P(("parts", "frame"), None, "tile", None),
            P("parts", None, None, None),
            P("parts", None, None, None),
        ),
        check_vma=False,
    )
```

profile of v0, /device:TPU:0, one launch (start us, length us, event | category | flops | bytes accessed | tf_op | source)
XLA Modules:
  0.0 316.0 jit_solution(6652373692335212695)
XLA Ops:
  9.5 3.5 %gather_fusion.1 = bf16[8,96,8,256]{3,2,1,0:T(8,128)(2,1)S(1)} fusion(bf16[16,96,8,256]{3,2,1,0:T(8,128)(2,1)} %param.10, s32[1024]{0:T(1024)S(1)} %pad_clamp_fusion), kind=kCustom, calls=%fused_computation.1.clone | custom fusion | bytes 6291488 | tf_op jit(solution)/shard_map/jit(_take)/gather | solution.py:100
  15.9 3.5 %gather_fusion = bf16[8,96,8,256]{3,2,1,0:T(8,128)(2,1)S(1)} fusion(bf16[16,96,8,256]{3,2,1,0:T(8,128)(2,1)} %param.10, s32[1024]{0:T(1024)S(1)} %pad_clamp_fusion.1), kind=kCustom, calls=%fused_computation.clone | custom fusion | bytes 6291488 | tf_op jit(solution)/shard_map/jit(_take)/gather | solution.py:105
  21.3 2.3 select_select_fusion.1
  25.4 4.8 %collective-permute-start.1 = (bf16[4,288,1,256]{3,1,2,0:T(8,128)(2,1)S(1)}, bf16[4,288,1,256]{3,1,2,0:T(8,128)(2,1)S(1)}, u32[]{:S(2)}, u32[]{:S(2)}) collective-permute-start(bf16[4,288,1,256]{3,1,2,0:T(8,128)(2,1)S(1)} %get-tuple-element.17), channel_id=1, source_target_pairs={{0,1},{1,2},{2,3},{3,4},{4,5},{5,6},{6,7},{8,9},{9,10},{10,11},{11... | collective-permute-start | bytes 1769480 | tf_op jit(solution)/shard_map/ppermute | solution.py:19
  31.8 3.0 fusion.184
  34.8 20.9 %collective-permute-done.1 = bf16[4,288,1,256]{3,1,2,0:T(8,128)(2,1)S(1)} collective-permute-done((bf16[4,288,1,256]{3,1,2,0:T(8,128)(2,1)S(1)}, bf16[4,288,1,256]{3,1,2,0:T(8,128)(2,1)S(1)}, u32[]{:S(2)}, u32[]{:S(2)}) %collective-permute-start.1) | collective-permute-done | bytes 589856 | tf_op jit(solution)/shard_map/ppermute | solution.py:19
  55.8 5.9 %fusion.5 = bf16[4,288,10,258]{3,1,2,0:T(8,128)(2,1)S(1)} fusion(bf16[4,288,1,256]{3,1,2,0:T(8,128)(2,1)S(1)} %collective-permute-done.2, bf16[4,288,8,256]{3,1,2,0:T(8,128)(2,1)S(1)} %copy_dynamic-update-slice_fusion.1, bf16[4,288,1,256]{3,1,2,0:T(8,128)(2,1)S(1)} %collective-permute-done.1), kind=kLoop, calls=%fused_computation.9 | loop fusion | flops 35665920 | bytes 11842560 | tf_op jit(solution)/shard_map/concatenate | solution.py:17
  61.7 3.0 fusion.13
  64.7 3.3 %fusion.17 = f32[4,8,256,96]{2,3,1,0:T(8,128)} fusion(bf16[4,288,10,258]{3,1,2,0:T(8,128)(2,1)S(1)} %fusion.5, bf16[3,3,96,288]{3,2,1,0:T(8,128)(2,1)S(1)} %copy-done.8), kind=kOutput, calls=%fused_computation.25 | convolution fusion | flops 452984832 | bytes 7938048 | tf_op jit(solution)/shard_map/oi,bihw->bohw/dot_general | solution.py:37
  68.0 3.0 fusion.21
  71.0 3.3 %fusion.25 = f32[4,8,256,96]{2,3,1,0:T(8,128)} fusion(bf16[4,288,10,258]{3,1,2,0:T(8,128)(2,1)S(1)} %fusion.5, bf16[3,3,96,288]{3,2,1,0:T(8,128)(2,1)S(1)} %copy-done.8), kind=kOutput, calls=%fused_computation.33 | convolution fusion | flops 452984832 | bytes 7938048 | tf_op jit(solution)/shard_map/oi,bihw->bohw/dot_general | solution.py:37
  74.3 3.0 fusion.29
  77.2 3.0 fusion.44
  80.3 3.0 fusion.42
  83.3 11.2 %fusion.38 = (bf16[4,96,8,256]{3,1,2,0:T(8,128)(2,1)}, f32[4,8,256,96]{2,3,1,0:T(8,128)}) fusion(bf16[4,288,10,258]{3,1,2,0:T(8,128)(2,1)S(1)} %fusion.5, bf16[3,3,96,288]{3,2,1,0:T(8,128)(2,1)} %param.16, f32[4,8,256,96]{2,3,1,0:T(8,128)} %fusion.44, f32[4,8,256,96]{2,3,1,0:T(8,128)} %fusion.13, f32[4,8,256,96]{2,3,1,0:T(8,128)} %fusion.17, ...), kind=kOutput, calls=%fused_computation.52 | convolution fusion | flops 463208448 | bytes 34676736 | tf_op jit(solution)/shard_map/oi,bihw->bohw/dot_general | solution.py:37
  95.6 4.4 %collective-permute-start.3 = (bf16[4,96,1,256]{3,1,2,0:T(8,128)(2,1)S(1)}, bf16[4,96,1,256]{3,1,2,0:T(8,128)(2,1)S(1)}, u32[]{:S(2)}, u32[]{:S(2)}) collective-permute-start(bf16[4,96,1,256]{3,1,2,0:T(8,128)(2,1)S(1)} %get-tuple-element.21), channel_id=1, source_target_pairs={{0,1},{1,2},{2,3},{3,4},{4,5},{5,6},{6,7},{8,9},{9,10},{10,11},{11... | collective-permute-start | bytes 589832 | tf_op jit(solution)/shard_map/ppermute | solution.py:19
  101.5 3.7 %fusion.209 = f32[4,8,256,96]{2,3,1,0:T(8,128)} fusion(bf16[4,96,8,256]{3,1,2,0:T(8,128)(2,1)} %get-tuple-element.25, bf16[3,3,96,96]{3,2,1,0:T(8,128)(2,1)S(1)} %copy-done.4), kind=kOutput, calls=%fused_computation.183 | convolution fusion | flops 150994944 | bytes 4743168 | tf_op jit(solution)/shard_map/oi,bihw->bohw/dot_general | solution.py:37
  105.2 3.9 %collective-permute-done.4 = bf16[4,96,1,256]{3,1,2,0:T(8,128)(2,1)S(1)} collective-permute-done((bf16[4,96,1,256]{3,1,2,0:T(8,128)(2,1)S(1)}, bf16[4,96,1,256]{3,1,2,0:T(8,128)(2,1)S(1)}, u32[]{:S(2)}, u32[]{:S(2)}) %collective-permute-start.4) | collective-permute-done | bytes 196640 | tf_op jit(solution)/shard_map/ppermute | solution.py:21
  113.3 2.4 fusion.80
  117.9 2.3 fusion.88
  126.9 12.3 %bitcast_convert_fusion = (bf16[4,96,8,256]{3,1,2,0:T(8,128)(2,1)}, f32[4,8,256,96]{2,3,1,0:T(8,128)}) fusion(bf16[4,96,10,258]{3,1,2,0:T(8,128)(2,1)S(1)} %select_maximum_fusion.2, bf16[3,3,96,96]{3,2,1,0:T(8,128)(2,1)S(1)} %copy-done.4, f32[4,8,256,96]{2,3,1,0:T(8,128)} %fusion.175, f32[4,8,256,96]{2,3,1,0:T(8,128)} %fusion.76, ...), kind=kOutput, calls=%fused_computation.42 | convolution fusion | flops 158072832 | bytes 31481856 | tf_op jit(solution)/shard_map/oi,bihw->bohw/dot_general | solution.py:37
  139.2 2.6 fusion.34
  146.0 5.6 %collective-permute-start.5 = (bf16[4,96,1,256]{3,1,2,0:T(8,128)(2,1)S(1)}, bf16[4,96,1,256]{3,1,2,0:T(8,128)(2,1)S(1)}, u32[]{:S(2)}, u32[]{:S(2)}) collective-permute-start(bf16[4,96,1,256]{3,1,2,0:T(8,128)(2,1)S(1)} %get-tuple-element.20), channel_id=1, source_target_pairs={{0,1},{1,2},{2,3},{3,4},{4,5},{5,6},{6,7},{8,9},{9,10},{10,11},{11... | collective-permute-start | bytes 589832 | tf_op jit(solution)/shard_map/ppermute | solution.py:19
  160.6 2.5 fusion.58
  163.1 2.3 fusion.60
  165.4 2.4 fusion.62
  170.1 2.5 fusion.66
  174.8 2.3 fusion.46
  177.1 10.5 %fusion.31 = bf16[4,96,8,256]{3,1,2,0:T(8,128)(2,1)S(1)} fusion(f32[4,8,256,96]{2,3,1,0:T(8,128)} %get-tuple-element.26, f32[4,8,256,96]{2,3,1,0:T(8,128)} %fusion.50, f32[4,8,256,96]{2,3,1,0:T(8,128)} %fusion.58, f32[4,8,256,96]{2,3,1,0:T(8,128)} %fusion.60, f32[4,8,256,96]{2,3,1,0:T(8,128)} %fusion.207, f32[4,8,256,96]{2,3,1,0:T(8,128)} %fusion.62, ...), kind=kOutput, calls=%fused_computation.40 | convolution fusion | flops 164364288 | bytes 31481856 | tf_op jit(solution)/shard_map/oi,bohw->bihw/dot_general | solution.py:66
  206.2 3.4 %copy.56 = bf16[4,96,8,256]{3,2,1,0:T(8,128)(2,1)} copy(bf16[4,96,8,256]{3,1,2,0:T(8,128)(2,1)} %get-tuple-element.27) | data formatting | bytes 3145728
  209.7 95.1 %all-reduce.6.cloned.1.call-done = (f32[3,3,96,288]{3,2,1,0:T(8,128)}, f32[3,3,96,96]{3,2,1,0:T(8,128)}) async-done(((f32[3,3,96,288]{3,2,1,0:T(8,128)}, f32[3,3,96,96]{3,2,1,0:T(8,128)}), (f32[3,3,96,288]{3,2,1,0:T(8,128)}, f32[3,3,96,96]{3,2,1,0:T(8,128)})) %all-reduce.6.cloned.1.call-update) | async-done | bytes 1327120 | tf_op jit(solution)/shard_map/psum | solution.py:130
  304.7 2.5 copy.133
  (89 shorter events, 63.9 us)
Async XLA Ops:
  7.2 297.6 %all-reduce.6.cloned.1.call-start = ((), (), s32[]{:S(2)}) async-start(), calls=%async_computation | async-start | bytes 3538944 | tf_op jit(solution)/shard_map/psum | solution.py:130
  13.1 2.6 copy-start.9
  15.2 6.1 %collective-permute-start = (bf16[8,96,8,256]{3,2,1,0:T(8,128)(2,1)}, bf16[8,96,8,256]{3,2,1,0:T(8,128)(2,1)}, u32[]{:S(2)}, u32[]{:S(2)}) collective-permute-start(bf16[8,96,8,256]{3,2,1,0:T(8,128)(2,1)} %select_select_fusion), channel_id=1, source_target_pairs={{0,8},{8,0},{1,9},{9,1},{2,10},{10,2},{3,11},{11,3},{4,12},{12,4},... | collective-permute-start | bytes 9437192 | tf_op jit(solution)/shard_map/ppermute | solution.py:8
  15.9 3.6 %copy-start.10 = (f32[32]{0:T(128)S(1)}, f32[32]{0:T(128)}, u32[]{:S(2)}) copy-start(f32[32]{0:T(128)} %param.15) | copy-start | bytes 388
  23.6 1.4 copy-start.1
  25.0 6.8 %copy-start.8 = (bf16[3,3,96,288]{3,2,1,0:T(8,128)(2,1)S(1)}, bf16[3,3,96,288]{3,2,1,0:T(8,128)(2,1)}, u32[]{:S(2)}) copy-start(bf16[3,3,96,288]{3,2,1,0:T(8,128)(2,1)} %param.16) | copy-start | bytes 1492996
  25.4 30.3 %collective-permute-start.1 = (bf16[4,288,1,256]{3,1,2,0:T(8,128)(2,1)S(1)}, bf16[4,288,1,256]{3,1,2,0:T(8,128)(2,1)S(1)}, u32[]{:S(2)}, u32[]{:S(2)}) collective-permute-start(bf16[4,288,1,256]{3,1,2,0:T(8,128)(2,1)S(1)} %get-tuple-element.17), channel_id=1, source_target_pairs={{0,1},{1,2},{2,3},{3,4},{4,5},{5,6},{6,7},{8,9},{9,10},{10,11},{11... | collective-permute-start | bytes 1769480 | tf_op jit(solution)/shard_map/ppermute | solution.py:19
  30.3 25.5 %collective-permute-start.2 = (bf16[4,288,1,256]{3,1,2,0:T(8,128)(2,1)S(1)}, bf16[4,288,1,256]{3,1,2,0:T(8,128)(2,1)S(1)}, u32[]{:S(2)}, u32[]{:S(2)}) collective-permute-start(bf16[4,288,1,256]{3,1,2,0:T(8,128)(2,1)S(1)} %get-tuple-element.18), channel_id=1, source_target_pairs={{1,0},{2,1},{3,2},{4,3},{5,4},{6,5},{7,6},{9,8},{10,9},{11,10},{12... | collective-permute-start | bytes 1769480 | tf_op jit(solution)/shard_map/ppermute | solution.py:21
  55.7 24.5 %copy-start.5 = (bf16[4,288,1,256]{3,1,2,0:T(8,128)(2,1)}, bf16[4,288,1,256]{3,1,2,0:T(8,128)(2,1)S(1)}, u32[]{:S(2)}) copy-start(bf16[4,288,1,256]{3,1,2,0:T(8,128)(2,1)S(1)} %collective-permute-done.1) | copy-start | bytes 1769476
  83.3 18.2 %copy-start.4 = (bf16[3,3,96,96]{3,2,1,0:T(8,128)(2,1)S(1)}, bf16[3,3,96,96]{3,2,1,0:T(8,128)(2,1)}, u32[]{:S(2)}) copy-start(bf16[3,3,96,96]{3,2,1,0:T(8,128)(2,1)} %param.17) | copy-start | bytes 497668
  94.4 14.7 %copy-start = (bf16[4,96,8,256]{3,1,2,0:T(8,128)(2,1)S(1)}, bf16[4,96,8,256]{3,1,2,0:T(8,128)(2,1)}, u32[]{:S(2)}) copy-start(bf16[4,96,8,256]{3,1,2,0:T(8,128)(2,1)} %get-tuple-element.25) | copy-start | bytes 4718596
  95.6 9.6 %collective-permute-start.3 = (bf16[4,96,1,256]{3,1,2,0:T(8,128)(2,1)S(1)}, bf16[4,96,1,256]{3,1,2,0:T(8,128)(2,1)S(1)}, u32[]{:S(2)}, u32[]{:S(2)}) collective-permute-start(bf16[4,96,1,256]{3,1,2,0:T(8,128)(2,1)S(1)} %get-tuple-element.21), channel_id=1, source_target_pairs={{0,1},{1,2},{2,3},{3,4},{4,5},{5,6},{6,7},{8,9},{9,10},{10,11},{11... | collective-permute-start | bytes 589832 | tf_op jit(solution)/shard_map/ppermute | solution.py:19
  100.0 9.1 %collective-permute-start.4 = (bf16[4,96,1,256]{3,1,2,0:T(8,128)(2,1)S(1)}, bf16[4,96,1,256]{3,1,2,0:T(8,128)(2,1)S(1)}, u32[]{:S(2)}, u32[]{:S(2)}) collective-permute-start(bf16[4,96,1,256]{3,1,2,0:T(8,128)(2,1)S(1)} %get-tuple-element.22), channel_id=1, source_target_pairs={{1,0},{2,1},{3,2},{4,3},{5,4},{6,5},{7,6},{9,8},{10,9},{11,10},{12... | collective-permute-start | bytes 589832 | tf_op jit(solution)/shard_map/ppermute | solution.py:21
  126.9 12.3 %copy-start.2 = (bf16[4,96,8,256]{3,2,1,0:T(8,128)(2,1)S(1)}, bf16[4,96,8,256]{3,2,1,0:T(8,128)(2,1)}, u32[]{:S(2)}) copy-start(bf16[4,96,8,256]{3,2,1,0:T(8,128)(2,1)} %param.11) | copy-start | bytes 4718596
  144.8 12.1 %collective-permute-start.6 = (bf16[4,96,1,256]{3,1,2,0:T(8,128)(2,1)S(1)}, bf16[4,96,1,256]{3,1,2,0:T(8,128)(2,1)S(1)}, u32[]{:S(2)}, u32[]{:S(2)}) collective-permute-start(bf16[4,96,1,256]{3,1,2,0:T(8,128)(2,1)S(1)} %get-tuple-element.19), channel_id=1, source_target_pairs={{1,0},{2,1},{3,2},{4,3},{5,4},{6,5},{7,6},{9,8},{10,9},{11,10},{12... | collective-permute-start | bytes 589832 | tf_op jit(solution)/shard_map/ppermute | solution.py:21
  146.0 12.6 %collective-permute-start.5 = (bf16[4,96,1,256]{3,1,2,0:T(8,128)(2,1)S(1)}, bf16[4,96,1,256]{3,1,2,0:T(8,128)(2,1)S(1)}, u32[]{:S(2)}, u32[]{:S(2)}) collective-permute-start(bf16[4,96,1,256]{3,1,2,0:T(8,128)(2,1)S(1)} %get-tuple-element.20), channel_id=1, source_target_pairs={{0,1},{1,2},{2,3},{3,4},{4,5},{5,6},{6,7},{8,9},{9,10},{10,11},{11... | collective-permute-start | bytes 589832 | tf_op jit(solution)/shard_map/ppermute | solution.py:19
  156.9 6.2 %copy-start.7 = (f32[9,96,96]{2,1,0:T(8,128)}, f32[9,96,96]{2,1,0:T(8,128)S(1)}, u32[]{:S(2)}) copy-start(f32[9,96,96]{2,1,0:T(8,128)S(1)} %fusion.168) | copy-start | bytes 995332
  187.7 1.8 copy-start.6
  205.1 1.1 copy-start.3
Sparse Core Ops, SparseCore 0:
  206.4 98.3 all-reduce.5
where the time goes:
time: 320 us; the launch traced here: 316 us
  waiting for transfers between devices  123 us (38%)
  matrix products  120 us (38%)
  local copies, waits for them, and re-layouts  20.6 us (6%)
  starting transfers between devices  19.6 us (6%)
  other arithmetic  18 us (6%)
  between operations  14.6 us (5%)
    psum x1, waiting for transfers between devices, on_device(): lax.psum((join_part, output_part), ('frame', 'tile'))  95.1 us
    dot_general x18, matrix products, apply_taps(): jnp.einsum('oi,bihw->bohw', kernel[row_tap, col_tap], window, preferred_e...  67.6 us
    dot_general x9, matrix products, transpose_taps(): jnp.einsum('oi,bohw->bihw', kernel[row_tap, col_tap], window, preferred_e...  29.3 us
    dot_general x18, matrix products, tap_grads(): jnp.einsum('bohw,bihw->oi', upstream, window, preferred_element_type=jnp....  23.1 us
    ppermute x3, waiting for transfers between devices, with_halo(): lax.ppermute(tail, axis, [(i, (i + 1) % count) for i in range(ends)])  22.7 us
    ppermute x3, starting transfers between devices, with_halo(): lax.ppermute(tail, axis, [(i, (i + 1) % count) for i in range(ends)])  14.8 us
    unnamed x26, local copies, waits for them, and re-layouts  10.2 us
    concatenate x3, other arithmetic, with_halo(): jnp.concatenate([lax.ppermute(tail, axis, [(i, (i + 1) % count) for i in...  9.9 us
  transfers between devices with their start and end apart: 8, of which 5 were waited for; matrix products, arithmetic and copies ran while one was open for 6% of the time, Pallas kernels for 0%

commit v1 on v0

v1 whole, which is shorter than its diff:
```python
import functools

import jax
import jax.numpy as jnp
from jax import lax
from jax.experimental import pallas as pl
from jax.experimental.pallas import tpu as pltpu
from jax.sharding import PartitionSpec as P

MESH = pl.DeviceIdType.MESH
BF16 = jnp.bfloat16
F32 = jnp.float32


def partner(array, axis, stride):
    return lax.ppermute(array, axis, [(i, i ^ 1 << stride) for i in range(lax.axis_size(axis))])


def dot(a, b):
    return jnp.dot(a, b, preferred_element_type=F32)


def from_left(v):
    lane = lax.broadcasted_iota(jnp.int32, v.shape, 1)
    return jnp.where(lane == 0, 0.0, pltpu.roll(v, 1, 1))


def from_right(v):
    cols = v.shape[1]
    lane = lax.broadcasted_iota(jnp.int32, v.shape, 1)
    return jnp.where(lane == cols - 1, 0.0, pltpu.roll(v, cols - 1, 1))


def join_cols(v, ch):
    return from_left(v[:ch]) + v[ch : 2 * ch] + from_right(v[2 * ch :])


def kernel(
    groups, tiles, scale_cells, wt, x, kj, ko, kt,
    recon_out, gout,
    pre, hid, resq, pgq, part_s, part_r, acc, s0, r0, s1, r1,
    hs, hr, s0s, s0r, s1s, s1r, gs, gr, ps, pr,
):
    frames, rows, cin, cols = x.shape
    ch = cin // 3
    chunk = gout.shape[1]
    f = lax.axis_index("frame")
    t = lax.axis_index("tile")
    other = 1 - f
    has_up = t > 0
    has_down = t < tiles - 1

    barrier = pltpu.get_barrier_semaphore()
    pl.semaphore_signal(barrier, inc=1, device_id={"frame": other}, device_id_type=MESH)
    for k in range(1, tiles):
        pl.semaphore_signal(
            barrier, inc=1, device_id={"tile": lax.rem(t + k, tiles)}, device_id_type=MESH
        )
    pl.semaphore_wait(barrier, tiles)

    def exchange(stage, to_up, up_slot, to_down, down_slot):
        up = pltpu.make_async_remote_copy(
            src_ref=to_up, dst_ref=up_slot, send_sem=hs.at[stage, 0], recv_sem=hr.at[stage, 0],
            device_id={"tile": lax.max(t - 1, 0)}, device_id_type=MESH,
        )
        down = pltpu.make_async_remote_copy(
            src_ref=to_down, dst_ref=down_slot, send_sem=hs.at[stage, 1], recv_sem=hr.at[stage, 1],
            device_id={"tile": lax.min(t + 1, tiles - 1)}, device_id_type=MESH,
        )

        @pl.when(has_up)
        def _():
            up.start()

        @pl.when(has_down)
        def _():
            down.start()

        def arrive():
            @pl.when(has_up)
            def _():
                down.wait_recv()
                up.wait_send()

            @pl.when(has_down)
            def _():
                up.wait_recv()
                down.wait_send()

        return arrive

    edge = jnp.zeros((frames, ch, cols), BF16)

    @pl.when(jnp.logical_not(has_up))
    def _():
        part_r[0] = edge
        hid[:, 0] = edge
        resq[1, :, 0] = edge
        pgq[1, :, 0] = edge

    @pl.when(jnp.logical_not(has_down))
    def _():
        part_r[1] = edge
        hid[:, rows + 1] = edge
        resq[1, :, rows + 1] = edge
        pgq[1, :, rows + 1] = edge

    @pl.loop(0, frames)
    def _(b):
        part_s[0, b] = join_cols(dot(kj[:, 2 * cin :], x[b, 0]), ch).astype(BF16)
        part_s[1, b] = join_cols(dot(kj[:, :cin], x[b, rows - 1]), ch).astype(BF16)

    acc[...] = jnp.zeros_like(acc)
    arrive = exchange(0, part_s.at[0], part_r.at[1], part_s.at[1], part_r.at[0])

    def activate(b, r, v):
        pre[b, r] = v
        hid[b, r + 1] = (v * jax.nn.sigmoid(v)).astype(BF16)

    @pl.loop(0, frames)
    def _(b):
        pre[b, 0] = join_cols(dot(kj[:, cin:], x[b, 0:2].reshape(2 * cin, cols)), ch)
        pre[b, rows - 1] = join_cols(
            dot(kj[:, : 2 * cin], x[b, rows - 2 : rows].reshape(2 * cin, cols)), ch
        )
        for r in range(1, rows - 1):
            v = join_cols(dot(kj[...], x[b, r - 1 : r + 2].reshape(3 * cin, cols)), ch)
            activate(b, r, v)

    arrive()

    @pl.loop(0, frames)
    def _(b):
        activate(b, 0, pre[b, 0] + part_r[0, b].astype(F32))
        activate(b, rows - 1, pre[b, rows - 1] + part_r[1, b].astype(F32))

    arrive = exchange(1, hid.at[:, 1], hid.at[:, rows + 1], hid.at[:, rows], hid.at[:, 0])

    def shifted(buf, b, r, v):
        buf[0, b, r] = from_right(v).astype(BF16)
        buf[2, b, r] = from_left(v).astype(BF16)

    def reconstruct(b, r):
        v = join_cols(dot(ko[...], hid[b, r : r + 3].reshape(3 * ch, cols)), ch)
        recon_out[b, r] = v.astype(BF16)
        current = x[b, r, 2 * ch :].astype(F32)
        res = (2.0 * wt[b] * (v - current) / scale_cells).astype(BF16)
        resq[1, b, r + 1] = res
        shifted(resq, b, r + 1, res.astype(F32))

    @pl.loop(0, frames)
    def _(b):
        for r in range(1, rows - 1):
            reconstruct(b, r)

    arrive()

    @pl.loop(0, frames)
    def _(b):
        reconstruct(b, 0)
        reconstruct(b, rows - 1)

    arrive = exchange(
        2, resq.at[1, :, 1], resq.at[1, :, rows + 1], resq.at[1, :, rows], resq.at[1, :, 0]
    )

    def through(b, r):
        hg = join_cols(dot(kt[...], resq[1, b, r : r + 3].reshape(3 * ch, cols)), ch)
        v = pre[b, r]
        s = jax.nn.sigmoid(v)
        pg = (hg * (s * (1.0 + v * (1.0 - s)))).astype(BF16)
        pgq[1, b, r + 1] = pg
        shifted(pgq, b, r + 1, pg.astype(F32))

    @pl.loop(0, frames)
    def _(b):
        for r in range(1, rows - 1):
            through(b, r)

    arrive()

    @pl.loop(0, frames)
    def _(b):
        through(b, 0)
        through(b, rows - 1)

    arrive = exchange(
        3, pgq.at[1, :, 1], pgq.at[1, :, rows + 1], pgq.at[1, :, rows], pgq.at[1, :, 0]
    )

    def ends(buf):
        @pl.loop(0, frames)
        def _(b):
            for r in (0, rows + 1):
                shifted(buf, b, r, buf[1, b, r].astype(F32))

    def row_band(get):
        return jnp.concatenate([get(r) for r in range(rows)], axis=1)

    def taps(buf, b):
        return jnp.concatenate(
            [
                row_band(lambda r: buf[q, b, r + 2 - p])
                for p in range(3)
                for q in range(3)
            ],
            axis=0,
        )

    def tap_dot(a, b):
        return lax.dot_general(a, b, (((1,), (1,)), ((), ())), preferred_element_type=F32)

    span = 9 * ch
    width = cin + ch
    low = cin // 128 * 128

    ends(resq)

    @pl.loop(0, frames)
    def _(b):
        base = row_band(lambda r: hid[b, r + 1])
        base = jnp.concatenate([jnp.zeros((cin - low, rows * cols), BF16), base], axis=0)
        acc[:span, low:] += tap_dot(taps(resq, b), base)

    arrive()
    ends(pgq)

    @pl.loop(0, frames)
    def _(b):
        base = row_band(lambda r: x[b, r])
        base = jnp.concatenate([base, jnp.zeros((ch, rows * cols), BF16)], axis=0)
        acc[:span] += tap_dot(taps(pgq, b), base)

    def rows_of(index):
        return pl.ds(pl.multiple_of(index * chunk, 8), chunk)

    def remote(src, dst, send, recv, **where):
        return pltpu.make_async_remote_copy(
            src_ref=src, dst_ref=dst, send_sem=send, recv_sem=recv,
            device_id=where, device_id_type=MESH,
        )

    order = [lax.rem(t + k, tiles) for k in range(1, tiles)] + [t]
    sends = []
    for d in order:
        s0[d] = acc[rows_of(other * tiles + d)].astype(BF16)
    for d in order:
        c = remote(s0.at[d], r0.at[d], s0s.at[d], s0r.at[d], frame=other)
        c.start()
        sends.append(c)
    total = None
    for i, d in enumerate(order):
        sends[i].wait_recv()
        v = acc[rows_of(f * tiles + d)] + r0[d].astype(F32)
        if i == tiles - 1:
            total = v
            break
        s1[d] = v.astype(BF16)
        c = remote(s1.at[d], r1.at[t], s1s.at[d], s1r.at[t], tile=d)
        c.start()
        sends.append(c)
    for d in order[:-1]:
        remote(s1.at[d], r1.at[d], s1s.at[d], s1r.at[d], tile=d).wait_recv()
        total = total + r1[d].astype(F32)
    mine = f * tiles + t
    gout[mine] = total.astype(BF16)
    for d in order[:-1]:
        c = remote(gout.at[mine], gout.at[mine], gs.at[d], gr.at[t], tile=d)
        c.start()
        sends.append(c)
    across = []
    for d in [t] + [lax.rem(t + tiles - k, tiles) for k in range(1, tiles)]:
        slot = f * tiles + d
        if across:
            remote(gout.at[slot], gout.at[slot], gs.at[d], gr.at[d], tile=d).wait_recv()
        c = remote(gout.at[slot], gout.at[slot], ps.at[d], pr.at[d], frame=other)
        c.start()
        across.append(c)
        sends.append(c)
    for d in order:
        slot = other * tiles + d
        remote(gout.at[slot], gout.at[slot], ps.at[d], pr.at[d], frame=other).wait_recv()
    for c in sends:
        c.wait_send()


def run_kernel(weights, x, kj, ko, kt, height):
    groups, tiles = lax.axis_size("frame"), lax.axis_size("tile")
    frames, rows, cin, cols = x.shape
    ch = cin // 3
    count = groups * tiles
    chunk = -(-9 * ch // (count * 8)) * 8
    width = cin + ch
    vm = pl.BlockSpec(memory_space=pltpu.VMEM)
    dma = pltpu.SemaphoreType.DMA
    return pl.pallas_call(
        functools.partial(kernel, groups, tiles, float(height * cols)),
        out_shape=(
            jax.ShapeDtypeStruct((frames, rows, ch, cols), BF16),
            jax.ShapeDtypeStruct((count, chunk, width), BF16),
        ),
        in_specs=[pl.BlockSpec(memory_space=pltpu.SMEM)] + [vm] * 4,
        out_specs=(vm, vm),
        scratch_shapes=[
            pltpu.VMEM((frames, rows, ch, cols), F32),
            pltpu.VMEM((frames, rows + 2, ch, cols), BF16),
            pltpu.VMEM((3, frames, rows + 2, ch, cols), BF16),
            pltpu.VMEM((3, frames, rows + 2, ch, cols), BF16),
            pltpu.VMEM((2, frames, ch, cols), BF16),
            pltpu.VMEM((2, frames, ch, cols), BF16),
            pltpu.VMEM((count * chunk, width), F32),
        ]
        + [pltpu.VMEM((tiles, chunk, width), BF16)] * 4
        + [dma((4, 2))] * 2
        + [dma((tiles,))] * 8,
        compiler_params=pltpu.CompilerParams(
            collective_id=0, has_side_effects=True, vmem_limit_bytes=60 * 2**20
        ),
    )(weights, x, kj, ko, kt)


def on_device(
    decoded_refs,
    current_frames,
    ref_pairs,
    ref_slots,
    frame_numbers,
    rate_weights,
    join_kernel,
    out_kernel,
):
    local_refs = decoded_refs.shape[0]
    local_frames, channels, tile_rows, col_count = current_frames.shape
    group = lax.axis_index("frame")
    frame_range = jnp.arange(ref_slots.shape[0], dtype=jnp.int32)

    def pair_slots(which):
        pairs = lax.dynamic_slice_in_dim(ref_pairs, which * local_frames, local_frames, 0)
        return jnp.sum(jnp.where(pairs[:, :, None] == frame_range, ref_slots, 0), axis=-1).reshape(
            -1
        )

    mine = pair_slots(group)
    other = pair_slots(1 - group) - group * local_refs
    outgoing = jnp.take(decoded_refs, jnp.clip(other, 0, local_refs - 1), axis=0)
    incoming = partner(outgoing, "frame", 0)
    mine_local = mine - group * local_refs
    mine_held = (mine_local >= 0) & (mine_local < local_refs)
    own_tiles = jnp.take(decoded_refs, jnp.clip(mine_local, 0, local_refs - 1), axis=0)
    picked = jnp.where(mine_held[:, None, None, None], own_tiles, incoming)
    picked = picked.reshape(local_frames, 2 * channels, tile_rows, col_count)
    stacked = jnp.concatenate([picked, current_frames], axis=1).transpose(0, 2, 1, 3)
    height = tile_rows * lax.axis_size("tile")

    frames_here = lax.dynamic_slice_in_dim(frame_numbers, group * local_frames, local_frames, 0)
    gop_range = jnp.arange(rate_weights.shape[0], dtype=jnp.int32)
    weight_here = jnp.sum(jnp.where(frames_here[:, None] == gop_range, rate_weights, 0.0), axis=-1)

    kj = join_kernel.transpose(1, 2, 0, 3).reshape(3 * channels, 9 * channels)
    ko = out_kernel.transpose(1, 2, 0, 3).reshape(3 * channels, 3 * channels)
    kt = out_kernel[::-1, ::-1].transpose(1, 3, 0, 2).reshape(3 * channels, 3 * channels)
    recon, grads = run_kernel(weight_here, stacked, kj, ko, kt, height)
    grads = grads.reshape(-1, 4 * channels)[: 9 * channels].astype(F32)
    grads = grads.reshape(3, 3, channels, 4 * channels)
    return (
        recon.transpose(0, 2, 1, 3),
        grads[..., : 3 * channels],
        grads[..., 3 * channels :],
    )


def solution(mesh):
    placed = (
        P(("parts", "frame"), None, "tile", None),
        P(("parts", "frame"), None, "tile", None),
        P("parts", None),
        P("parts"),
        P("parts"),
        P("parts"),
        P(),
        P(),
    )
    return jax.shard_map(
        on_device,
        mesh=mesh,
        in_specs=placed,
        out_specs=(
            P(("parts", "frame"), None, "tile", None),
            P("parts", None, None, None),
            P("parts", None, None, None),
        ),
        check_vma=False,
    )
```

time: 320 us -> 118 us (0.37)
  waiting for transfers between devices: 123 us -> 0.01 us
  matrix products: 120 us -> 0 us
  Pallas kernels: 0 us -> 80.2 us
  starting transfers between devices: 19.6 us -> 0.49 us
  between operations: 14.6 us -> 0.77 us
  other arithmetic: 18 us -> 8.46 us
  local copies, waits for them, and re-layouts: 20.6 us -> 27.2 us
    dot_general x45 -> x0, matrix products: 120 us -> none  [the longest x18 67.6 us: apply_taps(): jnp.einsum('oi,bihw->bohw', kernel[row_tap, col_tap], window, preferred_e...]
    psum x1 -> x0, waiting for transfers between devices: 95.1 us -> none  [on_device(): lax.psum((join_part, output_part), ('frame', 'tile'))]
    pallas_call x0 -> x1, Pallas kernels: none -> 80.2 us  [run_kernel(): pl.pallas_call(functools.partial(kernel, groups, tiles, float(height * co...]
    ppermute x6 -> x0, waiting for transfers between devices: 26.6 us -> none  [the longest x3 22.7 us: with_halo(): lax.ppermute(tail, axis, [(i, (i + 1) % count) for i in range(ends)])]
    ppermute x6 -> x0, starting transfers between devices: 19.1 us -> none  [the longest x3 14.8 us: with_halo(): lax.ppermute(tail, axis, [(i, (i + 1) % count) for i in range(ends)])]
    concatenate x3 -> x0, other arithmetic: 9.9 us -> none  [with_halo(): jnp.concatenate([lax.ppermute(tail, axis, [(i, (i + 1) % count) for i in...]
    reshape x0 -> x4, local copies, waits for them, and re-layouts: none -> 5.37 us  [the longest x1 2.87 us: on_device(): kj = join_kernel.transpose(1, 2, 0, 3).reshape(3 * channels, 9 * channels)]
    unnamed x26 -> x14, local copies, waits for them, and re-layouts: 10.2 us -> 5.69 us
  transfers between devices with their start and end apart: 8 -> 1, of which waited for: 5 -> 0; matrix products, arithmetic and copies ran while one was open for 6% -> 14% of each run, Pallas kernels for 0% -> 0%
where the time goes in v1:
time: 118 us; the launch traced here: 117 us
  Pallas kernels  80.2 us (68%)
  local copies, waits for them, and re-layouts  27.2 us (23%)
  other arithmetic  8.46 us (7%)
    pallas_call x1, Pallas kernels, run_kernel(): pl.pallas_call(functools.partial(kernel, groups, tiles, float(height * co...  80.2 us
    unnamed x14, local copies, waits for them, and re-layouts  5.69 us
    gather x1, local copies, waits for them, and re-layouts, on_device(): jnp.take(decoded_refs, jnp.clip(other, 0, local_refs - 1), axis=0)  3.54 us
    gather x1, local copies, waits for them, and re-layouts, on_device(): jnp.take(decoded_refs, jnp.clip(mine_local, 0, local_refs - 1), axis=0)  3.53 us
    reshape x1, local copies, waits for them, and re-layouts, on_device(): kj = join_kernel.transpose(1, 2, 0, 3).reshape(3 * channels, 9 * channels)  2.87 us
    transpose x1, other arithmetic, on_device(): jnp.concatenate([picked, current_frames], axis=1).transpose(0, 2, 1, 3)  2.47 us
  transfers between devices with their start and end apart: 1, of which 0 were waited for; matrix products, arithmetic and copies ran while one was open for 14% of the time, Pallas kernels for 0%

profile of v1, /device:TPU:0, one launch (start us, length us, event | category | flops | bytes accessed | tf_op | source)
XLA Modules:
  0.0 117.2 jit_solution(12090861480279804408)
XLA Ops:
  0.6 0.8 constant_dynamic-slice_fusion
  1.5 0.9 select_reduce_fusion.1
  2.3 0.1 copy.27
  2.4 0.1 min.18
  2.5 0.1 copy.28
  2.6 0.1 min.20
  2.8 3.5 %gather_fusion.1 = bf16[8,96,8,256]{3,2,1,0:T(8,128)(2,1)S(1)} fusion(bf16[16,96,8,256]{3,2,1,0:T(8,128)(2,1)} %param.10, s32[1024]{0:T(1024)S(1)} %pad_clamp_fusion), kind=kCustom, calls=%fused_computation.1.clone | custom fusion | bytes 6291488 | tf_op jit(solution)/shard_map/jit(_take)/gather | solution.py:345
  6.3 2.0 %broadcast_select_fusion = bf16[8,96,8,256]{3,2,1,0:T(8,128)(2,1)} fusion(bf16[8,96,8,256]{3,2,1,0:T(8,128)(2,1)S(1)} %gather_fusion.1, pred[8]{0:T(512)(128)(4,1)S(1)} %compare_and_fusion), kind=kLoop, calls=%fused_computation.4 | loop fusion | flops 1572864 | bytes 6291464 | tf_op jit(solution)/shard_map/jit(_take)/select_n | solution.py:345
  8.3 0.5 collective-permute-start
  8.8 3.5 %gather_fusion = bf16[8,96,8,256]{3,2,1,0:T(8,128)(2,1)S(1)} fusion(bf16[16,96,8,256]{3,2,1,0:T(8,128)(2,1)} %param.10, s32[1024]{0:T(1024)S(1)} %pad_clamp_fusion.1), kind=kCustom, calls=%fused_computation.clone | custom fusion | bytes 6291488 | tf_op jit(solution)/shard_map/jit(_take)/gather | solution.py:349
  12.3 0.0 copy-start.4
  12.4 0.1 copy.26
  12.5 0.1 and.16
  12.6 3.0 %copy.30 = bf16[4,96,8,256]{3,1,2,0:T(8,128)(2,1)} copy(bf16[4,96,8,256]{3,2,1,0:T(8,128)(2,1)} %param.11) | data formatting | bytes 3145728 | tf_op args[1]
  15.6 0.1 dynamic_slice.9
  15.7 1.4 %copy.31 = bf16[3,96,3,288]{3,2,1,0:T(4,128)(2,1)} copy(bf16[3,96,3,288]{3,1,0,2:T(8,128)(2,1)S(1)} %bitcast.16) | data formatting | bytes 995328 | tf_op jit(solution)/shard_map/transpose | solution.py:359
  17.0 2.9 %reshape.61.kj = bf16[288,864]{1,0:T(8,128)(2,1)} reshape(bf16[3,96,3,288]{3,2,1,0:T(4,128)(2,1)} %copy.31) | data formatting | bytes 995328 | tf_op jit(solution)/shard_map/reshape | solution.py:359
  19.9 0.7 reverse_bitcast_fusion
  20.6 1.1 copy.33
  21.7 0.9 reshape.63.kt
  22.6 1.1 copy.32
  23.7 0.9 reshape.62.ko
  24.6 0.8 select_reduce_fusion.2.wt
  25.4 2.3 %select_select_fusion = bf16[8,96,8,256]{3,2,1,0:T(8,128)(2,1)S(1)} fusion(bf16[8,96,8,256]{3,2,1,0:T(8,128)(2,1)} %collective-permute-done, bf16[8,96,8,256]{3,2,1,0:T(8,128)(2,1)S(1)} %gather_fusion, pred[8]{0:T(512)(128)(4,1)S(1)} %compare_and_fusion.1, pred[8]{0:T(512)(128)(4,1)S(1)} %and.16), kind=kLoop, calls=%fused_computation.3 | loop fusion | flops 3145728 | bytes 9437200 | tf_op jit(solution)/shard_map/jit(_where)/select_n | solution.py:350
  27.7 0.7 copy.29
  28.4 0.6 copy-done
  29.1 2.5 %maximum_bitcast_fusion.x = bf16[4,8,288,256]{3,2,1,0:T(8,128)(2,1)} fusion(bf16[4,96,8,256]{3,1,2,0:T(8,128)(2,1)S(1)} %copy-done, bf16[4,192,8,256]{3,1,2,0:T(8,128)(2,1)S(1)} %copy.29), kind=kLoop, calls=%fused_computation.2 | loop fusion | flops 9437184 | bytes 9437184 | tf_op jit(solution)/shard_map/transpose | solution.py:352
  31.5 80.2 %shard_map.103 = (bf16[4,8,96,256]{3,2,1,0:T(8,128)(2,1)}, bf16[16,56,384]{2,1,0:T(8,128)(2,1)}) custom-call(f32[4]{0:T(128)} %select_reduce_fusion.2.wt, bf16[4,8,288,256]{3,2,1,0:T(8,128)(2,1)} %maximum_bitcast_fusion.x, bf16[288,864]{1,0:T(8,128)(2,1)} %reshape.61.kj, bf16[288,288]{1,0:T(8,128)(2,1)} %reshape.62.ko, bf16[288,288]{1,0:T(8,128)(2,1)} %reshape.63.kt), custom_call_target="tpu_custom_call" | custom-call | tf_op jit(solution)/shard_map/pallas_call | solution.py:296
  111.8 1.3 %slice.16 = bf16[864,384]{1,0:T(8,128)(2,1)S(1)} slice(bf16[896,384]{1,0:T(8,128)(2,1)} %bitcast.17), slice={[0:864], [0:384]} | slice | bytes 1327104 | tf_op jit(solution)/shard_map/slice | solution.py:363
  113.1 1.2 %slice.17 = f32[3,3,96,288]{3,2,1,0:T(8,128)} slice(bf16[3,3,96,384]{3,2,1,0:T(8,128)(2,1)S(1)} %bitcast.12), slice={[0:3], [0:3], [0:96], [0:288]} | slice | bytes 1990656 | tf_op jit(solution)/shard_map/slice | solution.py:367
  114.2 0.9 slice.18
  115.1 2.0 %copy.34 = bf16[4,96,8,256]{3,2,1,0:T(8,128)(2,1)} copy(bf16[4,96,8,256]{3,1,2,0:T(8,128)(2,1)S(1)} %bitcast.14) | data formatting | bytes 3145728
  (19 shorter events, 0.1 us)
Async XLA Ops:
  8.3 17.0 %collective-permute-start = (bf16[8,96,8,256]{3,2,1,0:T(8,128)(2,1)}, bf16[8,96,8,256]{3,2,1,0:T(8,128)(2,1)}, u32[]{:S(2)}, u32[]{:S(2)}) collective-permute-start(bf16[8,96,8,256]{3,2,1,0:T(8,128)(2,1)} %broadcast_select_fusion), channel_id=1, source_target_pairs={{0,8},{8,0},{1,9},{9,1},{2,10},{10,2},{3,11},{11,3},{4,12},{12,4},... | collective-permute-start | bytes 9437192 | tf_op jit(solution)/shard_map/ppermute | solution.py:16
  12.3 3.2 %copy-start.4 = (s32[8]{0:T(128)S(1)}, s32[8]{0:T(128)}, u32[]{:S(2)}) copy-start(s32[8]{0:T(128)} %param.14) | copy-start | bytes 100
  12.4 7.5 %copy-start.2 = (bf16[3,3,96,96]{3,2,1,0:T(8,128)(2,1)S(1)}, bf16[3,3,96,96]{3,2,1,0:T(8,128)(2,1)}, u32[]{:S(2)}) copy-start(bf16[3,3,96,96]{3,2,1,0:T(8,128)(2,1)} %param.17) | copy-start | bytes 497668
  12.6 3.1 %copy-start.3 = (bf16[3,3,96,288]{3,2,1,0:T(8,128)(2,1)S(1)}, bf16[3,3,96,288]{3,2,1,0:T(8,128)(2,1)}, u32[]{:S(2)}) copy-start(bf16[3,3,96,288]{3,2,1,0:T(8,128)(2,1)} %param.16) | copy-start | bytes 1492996
  15.6 9.0 %copy-start.5 = (f32[32]{0:T(128)S(1)}, f32[32]{0:T(128)}, u32[]{:S(2)}) copy-start(f32[32]{0:T(128)} %param.15) | copy-start | bytes 388
  27.7 1.4 %copy-start = (bf16[4,96,8,256]{3,1,2,0:T(8,128)(2,1)S(1)}, bf16[4,96,8,256]{3,1,2,0:T(8,128)(2,1)}, u32[]{:S(2)}) copy-start(bf16[4,96,8,256]{3,1,2,0:T(8,128)(2,1)} %copy.30) | copy-start | bytes 4718596
  111.8 3.4 %copy-start.1 = (bf16[4,8,96,256]{3,2,1,0:T(8,128)(2,1)S(1)}, bf16[4,8,96,256]{3,2,1,0:T(8,128)(2,1)}, u32[]{:S(2)}) copy-start(bf16[4,8,96,256]{3,2,1,0:T(8,128)(2,1)} %get-tuple-element.6) | copy-start | bytes 4718596

commit v2 on v1

--- a/solution.py
+++ b/solution.py
@@ -36,9 +36,9 @@
 
 
 def kernel(
-    groups, tiles, scale_cells, wt, x, kj, ko, kt,
+    groups, tiles, scale_cells, wt, refs, current, kj_in, ko_in,
     recon_out, gout,
-    pre, hid, resq, pgq, part_s, part_r, acc, s0, r0, s1, r1,
+    x, kj, ko, kt, in_sem, pre, hid, resq, pgq, part_s, part_r, acc, s0, r0, s1, r1,
     hs, hr, s0s, s0r, s1s, s1r, gs, gr, ps, pr,
 ):
     frames, rows, cin, cols = x.shape
@@ -50,6 +50,16 @@
     has_up = t > 0
     has_down = t < tiles - 1
 
+    def load(b):
+        return (
+            pltpu.make_async_copy(refs.at[b], x.at[b, :, : 2 * ch], in_sem.at[b, 0]),
+            pltpu.make_async_copy(current.at[b], x.at[b, :, 2 * ch :], in_sem.at[b, 1]),
+        )
+
+    for b in range(frames):
+        for c in load(b):
+            c.start()
+
     barrier = pltpu.get_barrier_semaphore()
     pl.semaphore_signal(barrier, inc=1, device_id={"frame": other}, device_id_type=MESH)
     for k in range(1, tiles):
@@ -58,15 +68,28 @@
         )
     pl.semaphore_wait(barrier, tiles)
 
-    def exchange(stage, to_up, up_slot, to_down, down_slot):
+    def exchange(stage, b):
+        if stage == 0:
+            to_up, up_slot = part_s.at[0, b], part_r.at[1, b]
+            to_down, down_slot = part_s.at[1, b], part_r.at[0, b]
+        else:
+            buf = (hid, resq.at[1], pgq.at[1])[stage - 1]
+            to_up, up_slot = buf.at[b, 1], buf.at[b, rows + 1]
+            to_down, down_slot = buf.at[b, rows], buf.at[b, 0]
         up = pltpu.make_async_remote_copy(
-            src_ref=to_up, dst_ref=up_slot, send_sem=hs.at[stage, 0], recv_sem=hr.at[stage, 0],
+            src_ref=to_up, dst_ref=up_slot,
+            send_sem=hs.at[stage, b, 0], recv_sem=hr.at[stage, b, 0],
             device_id={"tile": lax.max(t - 1, 0)}, device_id_type=MESH,
         )
         down = pltpu.make_async_remote_copy(
-            src_ref=to_down, dst_ref=down_slot, send_sem=hs.at[stage, 1], recv_sem=hr.at[stage, 1],
+            src_ref=to_down, dst_ref=down_slot,
+            send_sem=hs.at[stage, b, 1], recv_sem=hr.at[stage, b, 1],
             device_id={"tile": lax.min(t + 1, tiles - 1)}, device_id_type=MESH,
         )
+        return up, down
+
+    def send(stage, b):
+        up, down = exchange(stage, b)
 
         @pl.when(has_up)
         def _():
@@ -76,18 +99,18 @@
         def _():
             down.start()
 
-        def arrive():
-            @pl.when(has_up)
-            def _():
-                down.wait_recv()
-                up.wait_send()
-
-            @pl.when(has_down)
-            def _():
-                up.wait_recv()
-                down.wait_send()
-
-        return arrive
+    def arrive(stage, b):
+        up, down = exchange(stage, b)
+
+        @pl.when(has_up)
+        def _():
+            down.wait_recv()
+            up.wait_send()
+
+        @pl.when(has_down)
+        def _():
+            up.wait_recv()
+            down.wait_send()
 
     edge = jnp.zeros((frames, ch, cols), BF16)
 
@@ -105,13 +128,22 @@
         resq[1, :, rows + 1] = edge
         pgq[1, :, rows + 1] = edge
 
-    @pl.loop(0, frames)
-    def _(b):
+    for p in range(3):
+        for q in range(3):
+            kj[q * ch : (q + 1) * ch, p * cin : (p + 1) * cin] = kj_in[p, q]
+            ko[q * ch : (q + 1) * ch, p * ch : (p + 1) * ch] = ko_in[p, q]
+            flipped = ko_in[2 - p, 2 - q].astype(F32).T.astype(BF16)
+            kt[q * ch : (q + 1) * ch, p * ch : (p + 1) * ch] = flipped
+
+    @pl.loop(0, frames)
+    def _(b):
+        for c in load(b):
+            c.wait()
         part_s[0, b] = join_cols(dot(kj[:, 2 * cin :], x[b, 0]), ch).astype(BF16)
         part_s[1, b] = join_cols(dot(kj[:, :cin], x[b, rows - 1]), ch).astype(BF16)
+        send(0, b)
 
     acc[...] = jnp.zeros_like(acc)
-    arrive = exchange(0, part_s.at[0], part_r.at[1], part_s.at[1], part_r.at[0])
 
     def activate(b, r, v):
         pre[b, r] = v
@@ -126,15 +158,10 @@
         for r in range(1, rows - 1):
             v = join_cols(dot(kj[...], x[b, r - 1 : r + 2].reshape(3 * cin, cols)), ch)
             activate(b, r, v)
-
-    arrive()
-
-    @pl.loop(0, frames)
-    def _(b):
+        arrive(0, b)
         activate(b, 0, pre[b, 0] + part_r[0, b].astype(F32))
         activate(b, rows - 1, pre[b, rows - 1] + part_r[1, b].astype(F32))
-
-    arrive = exchange(1, hid.at[:, 1], hid.at[:, rows + 1], hid.at[:, rows], hid.at[:, 0])
+        send(1, b)
 
     def shifted(buf, b, r, v):
         buf[0, b, r] = from_right(v).astype(BF16)
@@ -143,8 +170,8 @@
     def reconstruct(b, r):
         v = join_cols(dot(ko[...], hid[b, r : r + 3].reshape(3 * ch, cols)), ch)
         recon_out[b, r] = v.astype(BF16)
-        current = x[b, r, 2 * ch :].astype(F32)
-        res = (2.0 * wt[b] * (v - current) / scale_cells).astype(BF16)
+        target = x[b, r, 2 * ch :].astype(F32)
+        res = (2.0 * wt[b] * (v - target) / scale_cells).astype(BF16)
         resq[1, b, r + 1] = res
         shifted(resq, b, r + 1, res.astype(F32))
 
@@ -152,17 +179,10 @@
     def _(b):
         for r in range(1, rows - 1):
             reconstruct(b, r)
-
-    arrive()
-
-    @pl.loop(0, frames)
-    def _(b):
+        arrive(1, b)
         reconstruct(b, 0)
         reconstruct(b, rows - 1)
-
-    arrive = exchange(
-        2, resq.at[1, :, 1], resq.at[1, :, rows + 1], resq.at[1, :, rows], resq.at[1, :, 0]
-    )
+        send(2, b)
 
     def through(b, r):
         hg = join_cols(dot(kt[...], resq[1, b, r : r + 3].reshape(3 * ch, cols)), ch)
@@ -176,23 +196,14 @@
     def _(b):
         for r in range(1, rows - 1):
             through(b, r)
-
-    arrive()
-
-    @pl.loop(0, frames)
-    def _(b):
+        arrive(2, b)
         through(b, 0)
         through(b, rows - 1)
-
-    arrive = exchange(
-        3, pgq.at[1, :, 1], pgq.at[1, :, rows + 1], pgq.at[1, :, rows], pgq.at[1, :, 0]
-    )
-
-    def ends(buf):
-        @pl.loop(0, frames)
-        def _(b):
-            for r in (0, rows + 1):
-                shifted(buf, b, r, buf[1, b, r].astype(F32))
+        send(3, b)
+
+    def ends(buf, b):
+        for r in (0, rows + 1):
+            shifted(buf, b, r, buf[1, b, r].astype(F32))
 
     def row_band(get):
         return jnp.concatenate([get(r) for r in range(rows)], axis=1)
@@ -214,19 +225,17 @@
     width = cin + ch
     low = cin // 128 * 128
 
-    ends(resq)
-
-    @pl.loop(0, frames)
-    def _(b):
+    @pl.loop(0, frames)
+    def _(b):
+        ends(resq, b)
         base = row_band(lambda r: hid[b, r + 1])
         base = jnp.concatenate([jnp.zeros((cin - low, rows * cols), BF16), base], axis=0)
         acc[:span, low:] += tap_dot(taps(resq, b), base)
 
-    arrive()
-    ends(pgq)
-
-    @pl.loop(0, frames)
-    def _(b):
+    @pl.loop(0, frames)
+    def _(b):
+        arrive(3, b)
+        ends(pgq, b)
         base = row_band(lambda r: x[b, r])
         base = jnp.concatenate([base, jnp.zeros((ch, rows * cols), BF16)], axis=0)
         acc[:span] += tap_dot(taps(pgq, b), base)
@@ -284,10 +293,10 @@
         c.wait_send()
 
 
-def run_kernel(weights, x, kj, ko, kt, height):
+def run_kernel(weights, refs, current, join_kernel, out_kernel, height):
     groups, tiles = lax.axis_size("frame"), lax.axis_size("tile")
-    frames, rows, cin, cols = x.shape
-    ch = cin // 3
+    frames, rows, ch, cols = current.shape
+    cin = 3 * ch
     count = groups * tiles
     chunk = -(-9 * ch // (count * 8)) * 8
     width = cin + ch
@@ -299,9 +308,16 @@
             jax.ShapeDtypeStruct((frames, rows, ch, cols), BF16),
             jax.ShapeDtypeStruct((count, chunk, width), BF16),
         ),
-        in_specs=[pl.BlockSpec(memory_space=pltpu.SMEM)] + [vm] * 4,
+        in_specs=[pl.BlockSpec(memory_space=pltpu.SMEM)]
+        + [pl.BlockSpec(memory_space=pl.ANY)] * 2
+        + [vm] * 2,
         out_specs=(vm, vm),
         scratch_shapes=[
+            pltpu.VMEM((frames, rows, cin, cols), BF16),
+            pltpu.VMEM((cin, 3 * cin), BF16),
+            pltpu.VMEM((cin, cin), BF16),
+            pltpu.VMEM((cin, cin), BF16),
+            dma((frames, 2)),
             pltpu.VMEM((frames, rows, ch, cols), F32),
             pltpu.VMEM((frames, rows + 2, ch, cols), BF16),
             pltpu.VMEM((3, frames, rows + 2, ch, cols), BF16),
@@ -311,12 +327,12 @@
             pltpu.VMEM((count * chunk, width), F32),
         ]
         + [pltpu.VMEM((tiles, chunk, width), BF16)] * 4
-        + [dma((4, 2))] * 2
+        + [dma((4, frames, 2))] * 2
         + [dma((tiles,))] * 8,
         compiler_params=pltpu.CompilerParams(
             collective_id=0, has_side_effects=True, vmem_limit_bytes=60 * 2**20
         ),
-    )(weights, x, kj, ko, kt)
+    )(weights, refs, current, join_kernel, out_kernel)
 
 
 def on_device(
@@ -342,24 +358,22 @@
 
     mine = pair_slots(group)
     other = pair_slots(1 - group) - group * local_refs
-    outgoing = jnp.take(decoded_refs, jnp.clip(other, 0, local_refs - 1), axis=0)
+    outgoing = jnp.take(decoded_refs, jnp.clip(other, 0, local_refs - 1), axis=0, mode="clip")
     incoming = partner(outgoing, "frame", 0)
     mine_local = mine - group * local_refs
     mine_held = (mine_local >= 0) & (mine_local < local_refs)
-    own_tiles = jnp.take(decoded_refs, jnp.clip(mine_local, 0, local_refs - 1), axis=0)
+    own_tiles = jnp.take(decoded_refs, jnp.clip(mine_local, 0, local_refs - 1), axis=0, mode="clip")
     picked = jnp.where(mine_held[:, None, None, None], own_tiles, incoming)
     picked = picked.reshape(local_frames, 2 * channels, tile_rows, col_count)
-    stacked = jnp.concatenate([picked, current_frames], axis=1).transpose(0, 2, 1, 3)
+    refs = picked.transpose(0, 2, 1, 3)
+    current = current_frames.transpose(0, 2, 1, 3)
     height = tile_rows * lax.axis_size("tile")
 
     frames_here = lax.dynamic_slice_in_dim(frame_numbers, group * local_frames, local_frames, 0)
     gop_range = jnp.arange(rate_weights.shape[0], dtype=jnp.int32)
     weight_here = jnp.sum(jnp.where(frames_here[:, None] == gop_range, rate_weights, 0.0), axis=-1)
 
-    kj = join_kernel.transpose(1, 2, 0, 3).reshape(3 * channels, 9 * channels)
-    ko = out_kernel.transpose(1, 2, 0, 3).reshape(3 * channels, 3 * channels)
-    kt = out_kernel[::-1, ::-1].transpose(1, 3, 0, 2).reshape(3 * channels, 3 * channels)
-    recon, grads = run_kernel(weight_here, stacked, kj, ko, kt, height)
+    recon, grads = run_kernel(weight_here, refs, current, join_kernel, out_kernel, height)
     grads = grads.reshape(-1, 4 * channels)[: 9 * channels].astype(F32)
     grads = grads.reshape(3, 3, channels, 4 * channels)
     return (

time: 118 us -> 97.3 us (0.82)
  Pallas kernels: 80.2 us -> 71 us
  local copies, waits for them, and re-layouts: 27.2 us -> 20.9 us
  other arithmetic: 8.46 us -> 3.87 us
    pallas_call x1, Pallas kernels: 80.2 us -> 71 us  [run_kernel(): pl.pallas_call(functools.partial(kernel, groups, tiles, float(height * co...]
    reshape x3 -> x0, local copies, waits for them, and re-layouts: 4.63 us -> none  [the longest x1 2.87 us: on_device(): kj = join_kernel.transpose(1, 2, 0, 3).reshape(3 * channels, 9 * channels)]
    transpose x4 -> x0, local copies, waits for them, and re-layouts: 4.28 us -> none  [the longest x2 1.83 us: on_device(): out_kernel[::-1, ::-1].transpose(1, 3, 0, 2)]
    transpose x1 -> x0, other arithmetic: 2.47 us -> none  [on_device(): jnp.concatenate([picked, current_frames], axis=1).transpose(0, 2, 1, 3)]
    select_n x2 -> x0, other arithmetic: 2.02 us -> none  [on_device(): jnp.take(decoded_refs, jnp.clip(other, 0, local_refs - 1), axis=0)]
    gather x2, local copies, waits for them, and re-layouts: 7.07 us -> 8.75 us  [the longest x1 5.2 us: on_device(): jnp.take(decoded_refs, jnp.clip(other, 0, local_refs - 1), axis=0, mode='...]
    reshape x1, local copies, waits for them, and re-layouts: 0.75 us -> 2.41 us  [on_device(): picked = picked.reshape(local_frames, 2 * channels, tile_rows, col_count)]
    unnamed x14 -> x8, local copies, waits for them, and re-layouts: 5.69 us -> 4.97 us
  transfers between devices with their start and end apart: 1 -> 1, of which waited for: 0 -> 0; matrix products, arithmetic and copies ran while one was open for 14% -> 8% of each run, Pallas kernels for 0% -> 0%
where the time goes in v2:
time: 97.3 us; the launch traced here: 97 us
  Pallas kernels  71 us (73%)
  local copies, waits for them, and re-layouts  20.9 us (21%)
  other arithmetic  3.87 us (4%)
    pallas_call x1, Pallas kernels, run_kernel(): pl.pallas_call(functools.partial(kernel, groups, tiles, float(height * co...  71 us
    gather x1, local copies, waits for them, and re-layouts, on_device(): jnp.take(decoded_refs, jnp.clip(other, 0, local_refs - 1), axis=0, mode='...  5.2 us
    unnamed x8, local copies, waits for them, and re-layouts  4.97 us
    gather x1, local copies, waits for them, and re-layouts, on_device(): jnp.take(decoded_refs, jnp.clip(mine_local, 0, local_refs - 1), axis=0, m...  3.55 us
    reshape x1, local copies, waits for them, and re-layouts, on_device(): picked = picked.reshape(local_frames, 2 * channels, tile_rows, col_count)  2.41 us
    select_n x1, other arithmetic, on_device(): picked = jnp.where(mine_held[:, None, None, None], own_tiles, incoming)  2.28 us
  transfers between devices with their start and end apart: 1, of which 0 were waited for; matrix products, arithmetic and copies ran while one was open for 8% of the time, Pallas kernels for 0%

profile of v2, /device:TPU:0, one launch (start us, length us, event | category | flops | bytes accessed | tf_op | source)
XLA Modules:
  0.0 97.0 jit_solution(12588620202432945211)
XLA Ops:
  0.6 0.8 constant_dynamic-slice_fusion.1
  1.5 0.9 select_reduce_fusion
  2.4 0.1 copy.22
  2.4 0.1 reshape.90
  2.5 5.2 %gather_fusion.1 = bf16[8,96,8,256]{3,2,1,0:T(8,128)(2,1)} fusion(bf16[16,96,8,256]{3,2,1,0:T(8,128)(2,1)} %param.8, s32[1024]{0:T(1024)S(1)} %pad_clamp_fusion), kind=kCustom, calls=%fused_computation.1 | custom fusion | bytes 6291488 | tf_op jit(solution)/shard_map/jit(_take)/gather | solution.py:361
  7.7 0.5 collective-permute-start
  8.2 0.1 copy.21
  8.3 0.1 reshape.82
  8.4 0.0 copy-start.1
  8.4 3.5 %gather_fusion = bf16[8,96,8,256]{3,2,1,0:T(8,128)(2,1)S(1)} fusion(bf16[16,96,8,256]{3,2,1,0:T(8,128)(2,1)} %param.8, s32[1024]{0:T(1024)S(1)} %pad_clamp_fusion.1), kind=kCustom, calls=%fused_computation | custom fusion | bytes 6291488 | tf_op jit(solution)/shard_map/jit(_take)/gather | solution.py:365
  12.0 0.0 copy-start.2
  12.0 0.1 copy.20
  12.1 0.1 and.12
  12.2 0.0 copy-done.1
  12.2 0.1 dynamic_slice.9
  12.3 2.9 %copy.29 = bf16[4,96,8,256]{3,1,2,0:T(8,128)(2,1)} copy(bf16[4,96,8,256]{3,2,1,0:T(8,128)(2,1)} %param.9) | data formatting | bytes 3145728 | tf_op args[1]
  15.2 0.0 copy-done.2
  15.2 0.7 select_reduce_fusion.2.wt
  15.9 0.0 collective-permute-done
  15.9 2.3 %broadcast_select_fusion = bf16[8,96,8,256]{3,2,1,0:T(8,128)(2,1)S(1)} fusion(bf16[8,96,8,256]{3,2,1,0:T(8,128)(2,1)S(1)} %gather_fusion, bf16[8,96,8,256]{3,2,1,0:T(8,128)(2,1)} %collective-permute-done, pred[8]{0:T(512)(128)(4,1)S(1)} %and.12), kind=kLoop, calls=%fused_computation.3 | loop fusion | flops 1572864 | bytes 9437192 | tf_op jit(solution)/shard_map/jit(_where)/select_n | solution.py:366
  18.2 2.4 %copy.28 = bf16[4,192,8,256]{3,1,2,0:T(8,128)(2,1)} copy(bf16[4,192,8,256]{3,2,1,0:T(8,128)(2,1)S(1)} %bitcast.12) | data formatting | bytes 6291456 | tf_op jit(solution)/shard_map/reshape | solution.py:367
  20.6 71.0 %shard_map.103 = (bf16[4,8,96,256]{3,2,1,0:T(8,128)(2,1)}, bf16[16,56,384]{2,1,0:T(8,128)(2,1)}) custom-call(f32[4]{0:T(128)} %select_reduce_fusion.2.wt, bf16[4,8,192,256]{3,2,1,0:T(8,128)(2,1)} %bitcast.11, bf16[4,8,96,256]{3,2,1,0:T(8,128)(2,1)} %bitcast.15, bf16[3,3,96,288]{3,2,1,0:T(8,128)(2,1)} %kj_in.1, bf16[3,3,96,96]{3,2,1,0:T(8,128)(2,1)} %ko_in.1), custom_call_target="tpu_custom_call" | custom-call | tf_op jit(solution)/shard_map/pallas_call | solution.py:305
  91.6 0.0 copy-start
  91.6 1.3 %slice.16 = bf16[864,384]{1,0:T(8,128)(2,1)S(1)} slice(bf16[896,384]{1,0:T(8,128)(2,1)} %bitcast.17), slice={[0:864], [0:384]} | slice | bytes 1327104 | tf_op jit(solution)/shard_map/slice | solution.py:377
  92.9 1.2 %slice.17 = f32[3,3,96,288]{3,2,1,0:T(8,128)} slice(bf16[3,3,96,384]{3,2,1,0:T(8,128)(2,1)S(1)} %bitcast.13), slice={[0:3], [0:3], [0:96], [0:288]} | slice | bytes 1990656 | tf_op jit(solution)/shard_map/slice | solution.py:381
  94.0 0.9 slice.18
  94.9 0.0 copy-done
  94.9 2.0 %copy.25 = bf16[4,96,8,256]{3,2,1,0:T(8,128)(2,1)} copy(bf16[4,96,8,256]{3,1,2,0:T(8,128)(2,1)S(1)} %bitcast.16) | data formatting | bytes 3145728
  (4 shorter events, 0.0 us)
Async XLA Ops:
  7.7 8.2 %collective-permute-start = (bf16[8,96,8,256]{3,2,1,0:T(8,128)(2,1)}, bf16[8,96,8,256]{3,2,1,0:T(8,128)(2,1)}, u32[]{:S(2)}, u32[]{:S(2)}) collective-permute-start(bf16[8,96,8,256]{3,2,1,0:T(8,128)(2,1)} %gather_fusion.1), channel_id=1, source_target_pairs={{0,8},{8,0},{1,9},{9,1},{2,10},{10,2},{3,11},{11,3},{4,12},{12,4},... | collective-permute-start | bytes 9437192 | tf_op jit(solution)/shard_map/ppermute | solution.py:16
  8.4 3.8 %copy-start.1 = (s32[8]{0:T(128)S(1)}, s32[8]{0:T(128)}, u32[]{:S(2)}) copy-start(s32[8]{0:T(128)} %param.12) | copy-start | bytes 100
  12.0 3.2 %copy-start.2 = (f32[32]{0:T(128)S(1)}, f32[32]{0:T(128)}, u32[]{:S(2)}) copy-start(f32[32]{0:T(128)} %param.13) | copy-start | bytes 388
  91.6 3.4 %copy-start = (bf16[4,8,96,256]{3,2,1,0:T(8,128)(2,1)S(1)}, bf16[4,8,96,256]{3,2,1,0:T(8,128)(2,1)}, u32[]{:S(2)}) copy-start(bf16[4,8,96,256]{3,2,1,0:T(8,128)(2,1)} %get-tuple-element.5) | copy-start | bytes 4718596

commit v3 on v2

--- a/solution.py
+++ b/solution.py
@@ -236,59 +236,99 @@
     def _(b):
         arrive(3, b)
         ends(pgq, b)
-        base = row_band(lambda r: x[b, r])
+        base = row_band(lambda r: x[b, r, low:])
         base = jnp.concatenate([base, jnp.zeros((ch, rows * cols), BF16)], axis=0)
-        acc[:span] += tap_dot(taps(pgq, b), base)
+        acc[:span, low:] += tap_dot(taps(pgq, b), base)
 
     def rows_of(index):
         return pl.ds(pl.multiple_of(index * chunk, 8), chunk)
 
-    def remote(src, dst, send, recv, **where):
+    def remote(src, dst, send_sem, recv_sem, **where):
         return pltpu.make_async_remote_copy(
-            src_ref=src, dst_ref=dst, send_sem=send, recv_sem=recv,
+            src_ref=src, dst_ref=dst, send_sem=send_sem, recv_sem=recv_sem,
             device_id=where, device_id_type=MESH,
         )
 
     order = [lax.rem(t + k, tiles) for k in range(1, tiles)] + [t]
+    arrivals = [lax.rem(t + tiles - k, tiles) for k in range(1, tiles)]
+    mine = f * tiles + t
     sends = []
-    for d in order:
-        s0[d] = acc[rows_of(other * tiles + d)].astype(BF16)
-    for d in order:
-        c = remote(s0.at[d], r0.at[d], s0s.at[d], s0r.at[d], frame=other)
+
+    def start(c):
         c.start()
         sends.append(c)
-    total = None
-    for i, d in enumerate(order):
-        sends[i].wait_recv()
-        v = acc[rows_of(f * tiles + d)] + r0[d].astype(F32)
-        if i == tiles - 1:
-            total = v
-            break
-        s1[d] = v.astype(BF16)
-        c = remote(s1.at[d], r1.at[t], s1s.at[d], s1r.at[t], tile=d)
-        c.start()
-        sends.append(c)
-    for d in order[:-1]:
-        remote(s1.at[d], r1.at[d], s1s.at[d], s1r.at[d], tile=d).wait_recv()
-        total = total + r1[d].astype(F32)
-    mine = f * tiles + t
-    gout[mine] = total.astype(BF16)
-    for d in order[:-1]:
-        c = remote(gout.at[mine], gout.at[mine], gs.at[d], gr.at[t], tile=d)
-        c.start()
-        sends.append(c)
-    across = []
-    for d in [t] + [lax.rem(t + tiles - k, tiles) for k in range(1, tiles)]:
-        slot = f * tiles + d
-        if across:
-            remote(gout.at[slot], gout.at[slot], gs.at[d], gr.at[d], tile=d).wait_recv()
-        c = remote(gout.at[slot], gout.at[slot], ps.at[d], pr.at[d], frame=other)
-        c.start()
-        across.append(c)
-        sends.append(c)
-    for d in order:
-        slot = other * tiles + d
-        remote(gout.at[slot], gout.at[slot], ps.at[d], pr.at[d], frame=other).wait_recv()
+
+    def reduction(piece, first, last):
+        part = slice(first, last)
+
+        def to_core(d):
+            return remote(
+                s0.at[d, :, part], r0.at[d, :, part], s0s.at[piece, d], s0r.at[piece, d],
+                frame=other,
+            )
+
+        def to_tile(d, slot):
+            return remote(
+                s1.at[d, :, part], r1.at[slot, :, part], s1s.at[piece, d], s1r.at[piece, slot],
+                tile=d,
+            )
+
+        def result(slot, d, index):
+            held = gout.at[slot, :, part]
+            return remote(held, held, gs.at[piece, d], gr.at[piece, index], tile=d)
+
+        def across(slot, index):
+            held = gout.at[slot, :, part]
+            return remote(held, held, ps.at[piece, index], pr.at[piece, index], frame=other)
+
+        def exchange_cores():
+            for d in order:
+                s0[d, :, part] = acc[rows_of(other * tiles + d), part].astype(BF16)
+            for d in order:
+                start(to_core(d))
+
+        def scatter():
+            for d in order:
+                to_core(d).wait_recv()
+                v = acc[rows_of(f * tiles + d), part] + r0[d, :, part].astype(F32)
+                if d is t:
+                    acc[rows_of(mine), part] = v
+                else:
+                    s1[d, :, part] = v.astype(BF16)
+                    start(to_tile(d, t))
+
+        def gather():
+            total = acc[rows_of(mine), part]
+            for d in arrivals:
+                to_tile(d, d).wait_recv()
+                total = total + r1[d, :, part].astype(F32)
+            gout[mine, :, part] = total.astype(BF16)
+            for d in order[:-1]:
+                start(result(mine, d, t))
+            start(across(mine, t))
+
+        def forward():
+            for d in arrivals:
+                result(f * tiles + d, d, d).wait_recv()
+                start(across(f * tiles + d, d))
+
+        def finish():
+            for d in order:
+                across(other * tiles + d, d).wait_recv()
+
+        return [exchange_cores, scatter, gather, forward, finish]
+
+    steps = reduction(0, low, width)
+    steps.pop(0)()
+    for b in range(frames):
+        base = row_band(lambda r: x[b, r, :low])
+        acc[:span, :low] += tap_dot(taps(pgq, b), base)
+        if len(steps) > 1 and b < frames - 1:
+            steps.pop(0)()
+    last_steps = reduction(1, 0, low)
+    last_steps.pop(0)()
+    for step in steps + last_steps:
+        step()
     for c in sends:
         c.wait_send()
 
@@ -328,7 +368,7 @@
         ]
         + [pltpu.VMEM((tiles, chunk, width), BF16)] * 4
         + [dma((4, frames, 2))] * 2
-        + [dma((tiles,))] * 8,
+        + [dma((2, tiles))] * 8,
         compiler_params=pltpu.CompilerParams(
             collective_id=0, has_side_effects=True, vmem_limit_bytes=60 * 2**20
         ),
@@ -374,13 +414,11 @@
     weight_here = jnp.sum(jnp.where(frames_here[:, None] == gop_range, rate_weights, 0.0), axis=-1)
 
     recon, grads = run_kernel(weight_here, refs, current, join_kernel, out_kernel, height)
-    grads = grads.reshape(-1, 4 * channels)[: 9 * channels].astype(F32)
-    grads = grads.reshape(3, 3, channels, 4 * channels)
-    return (
-        recon.transpose(0, 2, 1, 3),
-        grads[..., : 3 * channels],
-        grads[..., 3 * channels :],
-    )
+    grads = grads.reshape(-1, 4 * channels)
+    inputs = 3 * channels
+    join_total = grads[: 9 * channels, :inputs].astype(F32).reshape(join_kernel.shape)
+    output_total = grads[: 9 * channels, inputs:].astype(F32).reshape(out_kernel.shape)
+    return (recon.transpose(0, 2, 1, 3), join_total, output_total)
 
 
 def solution(mesh):

time: 97.3 us -> 105 us (1.079)
  Pallas kernels: 71 us -> 78.1 us
  other arithmetic: 3.87 us -> 5.84 us
    pallas_call x1, Pallas kernels: 71 us -> 78.1 us  [run_kernel(): pl.pallas_call(functools.partial(kernel, groups, tiles, float(height * co...]
    reshape x0 -> x2, other arithmetic: none -> 1.97 us  [the longest x1 1.17 us: on_device(): grads[:9 * channels, :inputs].astype(F32).reshape(join_kernel.shape)]
    slice x3 -> x2, local copies, waits for them, and re-layouts: 3.34 us -> 2.33 us  [the longest x1 1.28 us: on_device(): grads[:9 * channels, :inputs].astype(F32).reshape(join_kernel.shape)]
  transfers between devices with their start and end apart: 1 -> 1, of which waited for: 0 -> 0; matrix products, arithmetic and copies ran while one was open for 8% -> 7% of each run, Pallas kernels for 0% -> 0%
where the time goes in v3:
time: 105 us
  Pallas kernels  78.1 us (74%)
  local copies, waits for them, and re-layouts  19.9 us (19%)
  other arithmetic  5.84 us (6%)
    pallas_call x1, Pallas kernels, run_kernel(): pl.pallas_call(functools.partial(kernel, groups, tiles, float(height * co...  78.1 us
    gather x1, local copies, waits for them, and re-layouts, on_device(): jnp.take(decoded_refs, jnp.clip(other, 0, local_refs - 1), axis=0, mode='...  5.2 us
    unnamed x8, local copies, waits for them, and re-layouts  4.97 us
    gather x1, local copies, waits for them, and re-layouts, on_device(): jnp.take(decoded_refs, jnp.clip(mine_local, 0, local_refs - 1), axis=0, m...  3.55 us
    reshape x1, local copies, waits for them, and re-layouts, on_device(): picked = picked.reshape(local_frames, 2 * channels, tile_rows, col_count)  2.41 us
    select_n x1, other arithmetic, on_device(): picked = jnp.where(mine_held[:, None, None, None], own_tiles, incoming)  2.28 us
  transfers between devices with their start and end apart: 1, of which 0 were waited for; matrix products, arithmetic and copies ran while one was open for 7% of the time, Pallas kernels for 0%

profile of v3, /device:TPU:0, one launch (start us, length us, event | category | flops | bytes accessed | tf_op | source)
XLA Modules:
  0.0 105.0 jit_solution(8552481069807980627)
XLA Ops:
  0.6 0.8 constant_dynamic-slice_fusion.1
  1.5 0.9 select_reduce_fusion
  2.4 0.1 copy.22
  2.4 0.1 reshape.100
  2.5 5.2 %gather_fusion.1 = bf16[8,96,8,256]{3,2,1,0:T(8,128)(2,1)} fusion(bf16[16,96,8,256]{3,2,1,0:T(8,128)(2,1)} %param.8, s32[1024]{0:T(1024)S(1)} %pad_clamp_fusion), kind=kCustom, calls=%fused_computation.1 | custom fusion | bytes 6291488 | tf_op jit(solution)/shard_map/jit(_take)/gather | solution.py:401
  7.7 0.5 collective-permute-start
  8.2 0.1 copy.21
  8.3 0.1 reshape.92
  8.4 0.0 copy-start.1
  8.4 3.5 %gather_fusion = bf16[8,96,8,256]{3,2,1,0:T(8,128)(2,1)S(1)} fusion(bf16[16,96,8,256]{3,2,1,0:T(8,128)(2,1)} %param.8, s32[1024]{0:T(1024)S(1)} %pad_clamp_fusion.1), kind=kCustom, calls=%fused_computation | custom fusion | bytes 6291488 | tf_op jit(solution)/shard_map/jit(_take)/gather | solution.py:405
  12.0 0.0 copy-start.2
  12.0 0.1 copy.20
  12.1 0.1 and.12
  12.2 0.0 copy-done.1
  12.2 0.1 dynamic_slice.9
  12.3 2.9 %copy.29 = bf16[4,96,8,256]{3,1,2,0:T(8,128)(2,1)} copy(bf16[4,96,8,256]{3,2,1,0:T(8,128)(2,1)} %param.9) | data formatting | bytes 3145728 | tf_op args[1]
  15.2 0.0 copy-done.2
  15.2 0.7 select_reduce_fusion.2.wt
  15.9 0.0 collective-permute-done
  15.9 2.3 %broadcast_select_fusion = bf16[8,96,8,256]{3,2,1,0:T(8,128)(2,1)S(1)} fusion(bf16[8,96,8,256]{3,2,1,0:T(8,128)(2,1)S(1)} %gather_fusion, bf16[8,96,8,256]{3,2,1,0:T(8,128)(2,1)} %collective-permute-done, pred[8]{0:T(512)(128)(4,1)S(1)} %and.12), kind=kLoop, calls=%fused_computation.3 | loop fusion | flops 1572864 | bytes 9437192 | tf_op jit(solution)/shard_map/jit(_where)/select_n | solution.py:406
  18.2 2.4 %copy.28 = bf16[4,192,8,256]{3,1,2,0:T(8,128)(2,1)} copy(bf16[4,192,8,256]{3,2,1,0:T(8,128)(2,1)S(1)} %bitcast.14) | data formatting | bytes 6291456 | tf_op jit(solution)/shard_map/reshape | solution.py:407
  20.6 78.1 %shard_map.103 = (bf16[4,8,96,256]{3,2,1,0:T(8,128)(2,1)}, bf16[16,56,384]{2,1,0:T(8,128)(2,1)}) custom-call(f32[4]{0:T(128)} %select_reduce_fusion.2.wt, bf16[4,8,192,256]{3,2,1,0:T(8,128)(2,1)} %bitcast.13, bf16[4,8,96,256]{3,2,1,0:T(8,128)(2,1)} %bitcast.15, bf16[3,3,96,288]{3,2,1,0:T(8,128)(2,1)} %kj_in.1, bf16[3,3,96,96]{3,2,1,0:T(8,128)(2,1)} %ko_in.1), custom_call_target="tpu_custom_call" | custom-call | tf_op jit(solution)/shard_map/pallas_call | solution.py:345
  98.7 0.0 copy-start
  98.7 1.3 %slice.12 = bf16[864,288]{1,0:T(8,128)(2,1)S(1)} slice(bf16[896,384]{1,0:T(8,128)(2,1)} %bitcast.18), slice={[0:864], [0:288]} | slice | bytes 995328 | tf_op jit(solution)/shard_map/slice | solution.py:419
  100.0 1.1 %slice.13 = bf16[864,96]{1,0:T(8,128)(2,1)S(1)} slice(bf16[896,384]{1,0:T(8,128)(2,1)} %bitcast.19), slice={[0:864], [288:384]} | slice | bytes 331776 | tf_op jit(solution)/shard_map/slice | solution.py:420
  101.0 1.2 %convert.2 = f32[3,3,96,288]{3,2,1,0:T(8,128)} convert(bf16[3,3,96,288]{3,2,1,0:T(8,128)(2,1)S(1)} %bitcast.16) | non-fusion elementwise | flops 248832 | bytes 1492992 | tf_op jit(solution)/shard_map/reshape | solution.py:419
  102.2 0.0 copy-done
  102.2 2.0 %copy.25 = bf16[4,96,8,256]{3,2,1,0:T(8,128)(2,1)} copy(bf16[4,96,8,256]{3,1,2,0:T(8,128)(2,1)S(1)} %bitcast.17) | data formatting | bytes 3145728
  104.2 0.8 convert.3
  (4 shorter events, 0.0 us)
Async XLA Ops:
  7.7 8.2 %collective-permute-start = (bf16[8,96,8,256]{3,2,1,0:T(8,128)(2,1)}, bf16[8,96,8,256]{3,2,1,0:T(8,128)(2,1)}, u32[]{:S(2)}, u32[]{:S(2)}) collective-permute-start(bf16[8,96,8,256]{3,2,1,0:T(8,128)(2,1)} %gather_fusion.1), channel_id=1, source_target_pairs={{0,8},{8,0},{1,9},{9,1},{2,10},{10,2},{3,11},{11,3},{4,12},{12,4},... | collective-permute-start | bytes 9437192 | tf_op jit(solution)/shard_map/ppermute | solution.py:16
  8.4 3.8 %copy-start.1 = (s32[8]{0:T(128)S(1)}, s32[8]{0:T(128)}, u32[]{:S(2)}) copy-start(s32[8]{0:T(128)} %param.12) | copy-start | bytes 100
  12.0 3.2 %copy-start.2 = (f32[32]{0:T(128)S(1)}, f32[32]{0:T(128)}, u32[]{:S(2)}) copy-start(f32[32]{0:T(128)} %param.13) | copy-start | bytes 388
  98.7 3.5 %copy-start = (bf16[4,8,96,256]{3,2,1,0:T(8,128)(2,1)S(1)}, bf16[4,8,96,256]{3,2,1,0:T(8,128)(2,1)}, u32[]{:S(2)}) copy-start(bf16[4,8,96,256]{3,2,1,0:T(8,128)(2,1)} %get-tuple-element.5) | copy-start | bytes 4718596

commit v4 on v2

--- a/solution.py
+++ b/solution.py
@@ -38,7 +38,7 @@
 def kernel(
     groups, tiles, scale_cells, wt, refs, current, kj_in, ko_in,
     recon_out, gout,
-    x, kj, ko, kt, in_sem, pre, hid, resq, pgq, part_s, part_r, acc, s0, r0, s1, r1,
+    x, kj, ko, kt, in_sem, pre, hid, resq, pgq, part_s, part_r, acc, acc_o, s0, r0, s1, r1,
     hs, hr, s0s, s0r, s1s, s1r, gs, gr, ps, pr,
 ):
     frames, rows, cin, cols = x.shape
@@ -144,6 +144,7 @@
         send(0, b)
 
     acc[...] = jnp.zeros_like(acc)
+    acc_o[...] = jnp.zeros_like(acc_o)
 
     def activate(b, r, v):
         pre[b, r] = v
@@ -222,23 +223,22 @@
         return lax.dot_general(a, b, (((1,), (1,)), ((), ())), preferred_element_type=F32)
 
     span = 9 * ch
-    width = cin + ch
-    low = cin // 128 * 128
 
     @pl.loop(0, frames)
     def _(b):
         ends(resq, b)
         base = row_band(lambda r: hid[b, r + 1])
-        base = jnp.concatenate([jnp.zeros((cin - low, rows * cols), BF16), base], axis=0)
-        acc[:span, low:] += tap_dot(taps(resq, b), base)
+        acc_o[...] += tap_dot(base, taps(resq, b))
 
     @pl.loop(0, frames)
     def _(b):
         arrive(3, b)
         ends(pgq, b)
         base = row_band(lambda r: x[b, r])
-        base = jnp.concatenate([base, jnp.zeros((ch, rows * cols), BF16)], axis=0)
-        acc[:span] += tap_dot(taps(pgq, b), base)
+        acc[:span, :cin] += tap_dot(taps(pgq, b), base)
+
+    for k in range(9):
+        acc[k * ch : (k + 1) * ch, cin:] = acc_o[:, k * ch : (k + 1) * ch].T
 
     def rows_of(index):
         return pl.ds(pl.multiple_of(index * chunk, 8), chunk)
@@ -325,6 +325,7 @@
             pltpu.VMEM((2, frames, ch, cols), BF16),
             pltpu.VMEM((2, frames, ch, cols), BF16),
             pltpu.VMEM((count * chunk, width), F32),
+            pltpu.VMEM((ch, 9 * ch), F32),
         ]
         + [pltpu.VMEM((tiles, chunk, width), BF16)] * 4
         + [dma((4, frames, 2))] * 2

time: 97.3 us -> 98.6 us (1.013)
  Pallas kernels: 71 us -> 72.3 us
    pallas_call x1, Pallas kernels: 71 us -> 72.3 us  [run_kernel(): pl.pallas_call(functools.partial(kernel, groups, tiles, float(height * co...]
where the time goes in v4:
time: 98.6 us; the launch traced here: 98.3 us
  Pallas kernels  72.3 us (73%)
  local copies, waits for them, and re-layouts  20.9 us (21%)
  other arithmetic  3.87 us (4%)
    pallas_call x1, Pallas kernels, run_kernel(): pl.pallas_call(functools.partial(kernel, groups, tiles, float(height * co...  72.3 us
    gather x1, local copies, waits for them, and re-layouts, on_device(): jnp.take(decoded_refs, jnp.clip(other, 0, local_refs - 1), axis=0, mode='...  5.2 us
    unnamed x8, local copies, waits for them, and re-layouts  4.97 us
    gather x1, local copies, waits for them, and re-layouts, on_device(): jnp.take(decoded_refs, jnp.clip(mine_local, 0, local_refs - 1), axis=0, m...  3.55 us
    reshape x1, local copies, waits for them, and re-layouts, on_device(): picked = picked.reshape(local_frames, 2 * channels, tile_rows, col_count)  2.41 us
    select_n x1, other arithmetic, on_device(): picked = jnp.where(mine_held[:, None, None, None], own_tiles, incoming)  2.28 us
  transfers between devices with their start and end apart: 1, of which 0 were waited for; matrix products, arithmetic and copies ran while one was open for 8% of the time, Pallas kernels for 0%

profile of v4, /device:TPU:0, one launch (start us, length us, event | category | flops | bytes accessed | tf_op | source)
XLA Modules:
  0.0 98.3 jit_solution(5055353045839289223)
XLA Ops:
  0.6 0.8 constant_dynamic-slice_fusion.1
  1.5 0.9 select_reduce_fusion
  2.4 0.1 copy.22
  2.4 0.1 reshape.90
  2.5 5.2 %gather_fusion.1 = bf16[8,96,8,256]{3,2,1,0:T(8,128)(2,1)} fusion(bf16[16,96,8,256]{3,2,1,0:T(8,128)(2,1)} %param.8, s32[1024]{0:T(1024)S(1)} %pad_clamp_fusion), kind=kCustom, calls=%fused_computation.1 | custom fusion | bytes 6291488 | tf_op jit(solution)/shard_map/jit(_take)/gather | solution.py:362
  7.7 0.5 collective-permute-start
  8.2 0.1 copy.21
  8.3 0.1 reshape.82
  8.4 0.0 copy-start.1
  8.4 3.5 %gather_fusion = bf16[8,96,8,256]{3,2,1,0:T(8,128)(2,1)S(1)} fusion(bf16[16,96,8,256]{3,2,1,0:T(8,128)(2,1)} %param.8, s32[1024]{0:T(1024)S(1)} %pad_clamp_fusion.1), kind=kCustom, calls=%fused_computation | custom fusion | bytes 6291488 | tf_op jit(solution)/shard_map/jit(_take)/gather | solution.py:366
  12.0 0.0 copy-start.2
  12.0 0.1 copy.20
  12.1 0.1 and.12
  12.2 0.0 copy-done.1
  12.2 0.1 dynamic_slice.9
  12.3 2.9 %copy.29 = bf16[4,96,8,256]{3,1,2,0:T(8,128)(2,1)} copy(bf16[4,96,8,256]{3,2,1,0:T(8,128)(2,1)} %param.9) | data formatting | bytes 3145728 | tf_op args[1]
  15.2 0.0 copy-done.2
  15.2 0.7 select_reduce_fusion.2.wt
  15.9 0.0 collective-permute-done
  15.9 2.3 %broadcast_select_fusion = bf16[8,96,8,256]{3,2,1,0:T(8,128)(2,1)S(1)} fusion(bf16[8,96,8,256]{3,2,1,0:T(8,128)(2,1)S(1)} %gather_fusion, bf16[8,96,8,256]{3,2,1,0:T(8,128)(2,1)} %collective-permute-done, pred[8]{0:T(512)(128)(4,1)S(1)} %and.12), kind=kLoop, calls=%fused_computation.3 | loop fusion | flops 1572864 | bytes 9437192 | tf_op jit(solution)/shard_map/jit(_where)/select_n | solution.py:367
  18.2 2.4 %copy.28 = bf16[4,192,8,256]{3,1,2,0:T(8,128)(2,1)} copy(bf16[4,192,8,256]{3,2,1,0:T(8,128)(2,1)S(1)} %bitcast.12) | data formatting | bytes 6291456 | tf_op jit(solution)/shard_map/reshape | solution.py:368
  20.6 72.3 %shard_map.103 = (bf16[4,8,96,256]{3,2,1,0:T(8,128)(2,1)}, bf16[16,56,384]{2,1,0:T(8,128)(2,1)}) custom-call(f32[4]{0:T(128)} %select_reduce_fusion.2.wt, bf16[4,8,192,256]{3,2,1,0:T(8,128)(2,1)} %bitcast.11, bf16[4,8,96,256]{3,2,1,0:T(8,128)(2,1)} %bitcast.15, bf16[3,3,96,288]{3,2,1,0:T(8,128)(2,1)} %kj_in.1, bf16[3,3,96,96]{3,2,1,0:T(8,128)(2,1)} %ko_in.1), custom_call_target="tpu_custom_call" | custom-call | tf_op jit(solution)/shard_map/pallas_call | solution.py:305
  92.9 0.0 copy-start
  92.9 1.3 %slice.16 = bf16[864,384]{1,0:T(8,128)(2,1)S(1)} slice(bf16[896,384]{1,0:T(8,128)(2,1)} %bitcast.17), slice={[0:864], [0:384]} | slice | bytes 1327104 | tf_op jit(solution)/shard_map/slice | solution.py:378
  94.2 1.2 %slice.17 = f32[3,3,96,288]{3,2,1,0:T(8,128)} slice(bf16[3,3,96,384]{3,2,1,0:T(8,128)(2,1)S(1)} %bitcast.13), slice={[0:3], [0:3], [0:96], [0:288]} | slice | bytes 1990656 | tf_op jit(solution)/shard_map/slice | solution.py:382
  95.4 0.9 slice.18
  96.3 0.0 copy-done
  96.3 2.0 %copy.25 = bf16[4,96,8,256]{3,2,1,0:T(8,128)(2,1)} copy(bf16[4,96,8,256]{3,1,2,0:T(8,128)(2,1)S(1)} %bitcast.16) | data formatting | bytes 3145728
  (4 shorter events, 0.0 us)
Async XLA Ops:
  7.7 8.2 %collective-permute-start = (bf16[8,96,8,256]{3,2,1,0:T(8,128)(2,1)}, bf16[8,96,8,256]{3,2,1,0:T(8,128)(2,1)}, u32[]{:S(2)}, u32[]{:S(2)}) collective-permute-start(bf16[8,96,8,256]{3,2,1,0:T(8,128)(2,1)} %gather_fusion.1), channel_id=1, source_target_pairs={{0,8},{8,0},{1,9},{9,1},{2,10},{10,2},{3,11},{11,3},{4,12},{12,4},... | collective-permute-start | bytes 9437192 | tf_op jit(solution)/shard_map/ppermute | solution.py:16
  8.4 3.8 %copy-start.1 = (s32[8]{0:T(128)S(1)}, s32[8]{0:T(128)}, u32[]{:S(2)}) copy-start(s32[8]{0:T(128)} %param.12) | copy-start | bytes 100
  12.0 3.2 %copy-start.2 = (f32[32]{0:T(128)S(1)}, f32[32]{0:T(128)}, u32[]{:S(2)}) copy-start(f32[32]{0:T(128)} %param.13) | copy-start | bytes 388
  92.9 3.4 %copy-start = (bf16[4,8,96,256]{3,2,1,0:T(8,128)(2,1)S(1)}, bf16[4,8,96,256]{3,2,1,0:T(8,128)(2,1)}, u32[]{:S(2)}) copy-start(bf16[4,8,96,256]{3,2,1,0:T(8,128)(2,1)} %get-tuple-element.5) | copy-start | bytes 4718596
